TPU v7x, 8 devices: a whole 2x2x1 slice. The times are simulated.
8 devices in a mesh: hp: 4 (over z, y, x), cp: 2 (over core).
Axes of the slice: x: 2, y: 2, z: 1, core: 2. Of those that a mesh axis runs over, the one named last changes fastest.
Arguments:
- hidden: bfloat16 [2048, 2048], P(('cp', 'hp'))
- grad_out: bfloat16 [2048, 2048], P(('cp', 'hp'))
- positions: int32 [2048], P(('cp', 'hp'))
- norm_gain: bfloat16 [2048], replicated
- w_q: bfloat16 [2048, 2048], replicated
- w_k: bfloat16 [2048, 256], replicated
- w_v: bfloat16 [2048, 256], replicated
- w_o: bfloat16 [2048, 2048], replicated
- inv_freq: float32 [32], replicated
Outputs:
- output 1: bfloat16 [2048, 2048], P(('cp', 'hp'))
- output 2: bfloat16 [2048, 2048], P(('cp', 'hp'))
- output 3: float32 [2048, 2048], replicated
- output 4: float32 [2048, 256], replicated
- output 5: float32 [2048, 256], replicated
- output 6: float32 [2048, 2048], replicated
- output 7: float32 [2048], replicated
All inputs are finite; a program needn't handle non-finite values.
Results may differ from a plain program's by a relative error of at most 0.00983856.
Values are sent between devices in bfloat16 or wider.
A program may use at most 1 GiB of HBM per device.

v0:
```python
import jax
import jax.numpy as jnp
from jax import lax
from jax.sharding import PartitionSpec as P

NORM_EPS = 1e-5


def rope_apply(vectors, cos_t, sin_t):
    half_dim = vectors.shape[-1] // 2
    lo_half = vectors[..., :half_dim]
    hi_half = vectors[..., half_dim:]
    return jnp.concatenate([lo_half * cos_t - hi_half * sin_t, hi_half * cos_t + lo_half * sin_t], axis=-1)


def rope_undo(vectors, cos_t, sin_t):
    half_dim = vectors.shape[-1] // 2
    lo_half = vectors[..., :half_dim]
    hi_half = vectors[..., half_dim:]
    return jnp.concatenate([lo_half * cos_t + hi_half * sin_t, hi_half * cos_t - lo_half * sin_t], axis=-1)


def pair_index(pair_id, n_pairs, pair_rows):
    block_len = pair_rows // 2
    within = jnp.arange(pair_rows, dtype=jnp.int32)
    return jnp.where(within < block_len, pair_id * block_len + within, (2 * n_pairs - 1 - pair_id) * block_len + within - block_len)


def stored_index(n_pairs, pair_rows):
    block_len = pair_rows // 2
    rows_idx = jnp.arange(n_pairs * pair_rows, dtype=jnp.int32)
    pair_id = rows_idx // pair_rows
    within = rows_idx % pair_rows
    return jnp.where(within < block_len, pair_id * block_len + within, (2 * n_pairs - 1 - pair_id) * block_len + within - block_len)


def solution(mesh):
    hp_size = mesh.shape['hp']
    cp_size = mesh.shape['cp']

    def device_step(hidden, grad_out, positions, norm_gain, w_q, w_k, w_v, w_o, inv_freq):
        tok_rows = hidden.shape[0]
        head_dim = 2 * inv_freq.shape[0]
        n_heads = w_q.shape[1] // head_dim
        n_kv = w_k.shape[1] // head_dim
        repeat = max(1, hp_size // n_kv)
        loc_heads = n_heads // hp_size
        loc_kv = n_kv * repeat // hp_size
        loc_group = loc_heads // loc_kv
        pair_rows = tok_rows * hp_size
        score_scale = head_dim ** -0.5
        cp_idx = lax.axis_index('cp')
        x_f32 = hidden.astype(jnp.float32)
        inv_rms = lax.rsqrt(jnp.mean(x_f32 * x_f32, axis=-1, keepdims=True) + NORM_EPS)
        x_hat = x_f32 * inv_rms
        normed = (x_hat * norm_gain.astype(jnp.float32)).astype(jnp.bfloat16)
        angles = positions.astype(jnp.float32)[:, None] * inv_freq[None, :]
        cos_t = jnp.cos(angles)[:, None, :]
        sin_t = jnp.sin(angles)[:, None, :]
        q_rot = rope_apply(jnp.dot(normed, w_q, preferred_element_type=jnp.float32).reshape(tok_rows, n_heads, head_dim), cos_t, sin_t).astype(jnp.bfloat16)
        k_rot = rope_apply(jnp.dot(normed, w_k, preferred_element_type=jnp.float32).reshape(tok_rows, n_kv, head_dim), cos_t, sin_t).astype(jnp.bfloat16)
        v_val = jnp.dot(normed, w_v, preferred_element_type=jnp.float32).astype(jnp.bfloat16).reshape(tok_rows, n_kv, head_dim)
        if repeat > 1:
            k_rot = jnp.repeat(k_rot, repeat, axis=1)
            v_val = jnp.repeat(v_val, repeat, axis=1)
        q_head = lax.all_to_all(q_rot, 'hp', 1, 0, tiled=True).reshape(pair_rows, loc_kv, loc_group, head_dim)
        k_head = lax.all_to_all(k_rot, 'hp', 1, 0, tiled=True)
        v_head = lax.all_to_all(v_val, 'hp', 1, 0, tiled=True)
        k_all = lax.all_gather(k_head, 'cp', axis=0, tiled=True)
        v_all = lax.all_gather(v_head, 'cp', axis=0, tiled=True)
        q_idx = pair_index(cp_idx, cp_size, pair_rows)
        k_idx = stored_index(cp_size, pair_rows)
        visible = q_idx[:, None] >= k_idx[None, :]
        scores = jnp.einsum('qkgd,tkd->kgqt', q_head, k_all, preferred_element_type=jnp.float32) * score_scale
        scores = jnp.where(visible, scores, -1e30)
        prob_f32 = jnp.exp(scores - jnp.max(scores, axis=-1, keepdims=True))
        prob_f32 = prob_f32 / jnp.sum(prob_f32, axis=-1, keepdims=True)
        prob_b16 = prob_f32.astype(jnp.bfloat16)
        out_head = jnp.einsum('kgqt,tkd->qkgd', prob_b16, v_all, preferred_element_type=jnp.float32).astype(jnp.bfloat16)
        attn_out = lax.all_to_all(out_head.reshape(pair_rows, loc_heads, head_dim), 'hp', 0, 1, tiled=True).reshape(tok_rows, n_heads * head_dim)
        output = (x_f32 + jnp.dot(attn_out, w_o, preferred_element_type=jnp.float32)).astype(jnp.bfloat16)
        grad_wo = jnp.einsum('ta,tb->ab', attn_out, grad_out, preferred_element_type=jnp.float32)
        d_out = jnp.einsum('tb,ab->ta', grad_out, w_o, preferred_element_type=jnp.float32).astype(jnp.bfloat16).reshape(tok_rows, n_heads, head_dim)
        do_head = lax.all_to_all(d_out, 'hp', 1, 0, tiled=True).reshape(pair_rows, loc_kv, loc_group, head_dim)
        row_delta = jnp.einsum('qkgd,qkgd->kgq', do_head, out_head, preferred_element_type=jnp.float32)
        d_prob = jnp.einsum('qkgd,tkd->kgqt', do_head, v_all, preferred_element_type=jnp.float32)
        d_score = (prob_f32 * (d_prob - row_delta[..., None])).astype(jnp.bfloat16)
        dq_head = (jnp.einsum('kgqt,tkd->qkgd', d_score, k_all, preferred_element_type=jnp.float32) * score_scale).astype(jnp.bfloat16)
        dk_part = (jnp.einsum('kgqt,qkgd->tkd', d_score, q_head, preferred_element_type=jnp.float32) * score_scale).astype(jnp.bfloat16)
        dv_part = jnp.einsum('kgqt,qkgd->tkd', prob_b16, do_head, preferred_element_type=jnp.float32).astype(jnp.bfloat16)
        dk_head = lax.psum_scatter(dk_part, 'cp', scatter_dimension=0, tiled=True)
        dv_head = lax.psum_scatter(dv_part, 'cp', scatter_dimension=0, tiled=True)
        dq_seq = lax.all_to_all(dq_head.reshape(pair_rows, loc_heads, head_dim), 'hp', 0, 1, tiled=True)
        dk_seq = lax.all_to_all(dk_head, 'hp', 0, 1, tiled=True)
        dv_seq = lax.all_to_all(dv_head, 'hp', 0, 1, tiled=True)
        if repeat > 1:
            dk_seq = jnp.sum(dk_seq.reshape(tok_rows, n_kv, repeat, head_dim).astype(jnp.float32), axis=2).astype(jnp.bfloat16)
            dv_seq = jnp.sum(dv_seq.reshape(tok_rows, n_kv, repeat, head_dim).astype(jnp.float32), axis=2).astype(jnp.bfloat16)
        g_q = rope_undo(dq_seq.astype(jnp.float32), cos_t, sin_t).astype(jnp.bfloat16).reshape(tok_rows, n_heads * head_dim)
        g_k = rope_undo(dk_seq.astype(jnp.float32), cos_t, sin_t).astype(jnp.bfloat16).reshape(tok_rows, n_kv * head_dim)
        g_v = dv_seq.reshape(tok_rows, n_kv * head_dim)
        grad_wq = jnp.einsum('ta,tb->ab', normed, g_q, preferred_element_type=jnp.float32)
        grad_wk = jnp.einsum('ta,tb->ab', normed, g_k, preferred_element_type=jnp.float32)
        grad_wv = jnp.einsum('ta,tb->ab', normed, g_v, preferred_element_type=jnp.float32)
        d_norm = jnp.einsum('tb,ab->ta', g_q, w_q, preferred_element_type=jnp.float32) + jnp.einsum('tb,ab->ta', g_k, w_k, preferred_element_type=jnp.float32) + jnp.einsum('tb,ab->ta', g_v, w_v, preferred_element_type=jnp.float32)
        grad_gain = jnp.sum(d_norm * x_hat, axis=0)
        d_hat = d_norm * norm_gain.astype(jnp.float32)
        grad_hidden = (grad_out.astype(jnp.float32) + inv_rms * (d_hat - x_hat * jnp.mean(d_hat * x_hat, axis=-1, keepdims=True))).astype(jnp.bfloat16)
        weight_grads = lax.psum((grad_wq, grad_wk, grad_wv, grad_wo, grad_gain), ('hp', 'cp'))
        return (output, grad_hidden) + tuple(weight_grads)

    seq_spec = P(('cp', 'hp'), None)
    whole = P()
    return jax.shard_map(device_step, mesh=mesh, in_specs=(seq_spec, seq_spec, P(('cp', 'hp')), whole, whole, whole, whole, whole, whole), out_specs=(seq_spec, seq_spec, whole, whole, whole, whole, whole), check_vma=False)
```

profile of v0, /device:TPU:0, one launch (start us, length us, event | category | flops | bytes accessed | tf_op | source)
XLA Modules:
  0.0 794.1 jit_solution(7249402983801739641)
XLA Ops:
  9.6 2.6 convolution_convert_fusion.1
  12.1 5.7 all-to-all-start
  20.7 2.0 all-to-all-done
  22.6 3.3 all-to-all-start.1
  26.0 6.7 convolution_convert_fusion
  32.7 2.3 copy.66
  35.0 4.2 all-to-all-start.4
  39.1 6.9 fusion.67
  47.4 3.4 all-to-all-done.4
  50.8 4.3 all-to-all-start.2
  56.6 1.9 all_gather.6
  58.5 2.5 all_gather.7
  62.8 2.6 reshape.224
  65.4 2.7 all-to-all-done.2
  68.1 3.0 copy.96
  71.1 2.6 reshape.219
  73.7 25.0 %fusion.4 = (f32[8,1024]{1,0:T(8,128)S(1)}, f32[2048,1024,8]{1,0,2:T(8,128)}) fusion(pred[1024,2048]{0,1:T(8,128)(4,1)S(1)} %broadcast_compare_fusion, bf16[1024,8,64]{0,2,1:T(8,128)(2,1)} %reshape.219, bf16[2048,1,64]{0,2,1:T(8,128)(2,1)S(1)} %all_gather.7), kind=kOutput, calls=%fused_computation.7 | convolution fusion | flops 2197807104 | bytes 70549504 | tf_op jit(solution)/shard_map/qkgd,tkd->kgqt/dot_general | solution.py:74
  98.6 21.5 %fusion.3 = f32[8,1024]{1,0:T(8,128)S(1)} fusion(f32[2048,1024,8]{1,0,2:T(8,128)} %get-tuple-element.24, f32[8,1024]{1,0:T(8,128)S(1)} %get-tuple-element.23, pred[1024,2048]{0,1:T(8,128)(4,1)S(1)} %broadcast_compare_fusion), kind=kLoop, calls=%fused_computation.6 | loop fusion | flops 67100672 | bytes 69271552 | tf_op jit(solution)/shard_map/reduce_sum | solution.py:77
  120.2 27.3 %fusion.24 = bf16[2048,1,64]{0,2,1:T(8,128)(2,1)} fusion(bf16[1024,8,64]{0,2,1:T(8,128)(2,1)} %reshape.224, f32[8,1024]{1,0:T(8,128)S(1)} %fusion.3, f32[8,1024]{1,0:T(8,128)S(1)} %get-tuple-element.23, f32[2048,1024,8]{1,0,2:T(8,128)} %get-tuple-element.24, pred[1024,2048]{0,1:T(8,128)(4,1)S(1)} %broadcast_compare_fusion), kind=kOutput, calls=%fused_computation.31 | convolution fusion | flops 2231500800 | bytes 70582272 | tf_op jit(solution)/shard_map/kgqt,qkgd->tkd/dot_general | solution.py:90
  147.7 32.6 %fusion.36 = (f32[8,1024]{1,0:T(8,128)S(1)}, bf16[64,8,1024]{2,0,1:T(8,128)(2,1)}) fusion(bf16[1024,8,64]{0,2,1:T(8,128)(2,1)} %reshape.224, f32[8,1024]{1,0:T(8,128)S(1)} %fusion.3, f32[8,1024]{1,0:T(8,128)S(1)} %get-tuple-element.23, f32[2048,1024,8]{1,0,2:T(8,128)} %get-tuple-element.24, pred[1024,2048]{0,1:T(8,128)(4,1)S(1)} %broadcast_compare_fusion, ...), kind=kOutput, calls=%fused_computation.42 | convolution fusion | flops 2233982976 | bytes 71663616 | tf_op jit(solution)/shard_map/kgqt,tkd->qkgd/dot_general | solution.py:79
  180.3 38.9 %fusion.5 = bf16[8,1024,2048]{1,2,0:T(8,128)(2,1)} fusion(f32[8,1024]{1,0:T(8,128)S(1)} %get-tuple-element.25, f32[8,1024]{1,0:T(8,128)S(1)} %fusion.3, f32[8,1024]{1,0:T(8,128)S(1)} %get-tuple-element.23, f32[2048,1024,8]{1,0,2:T(8,128)} %get-tuple-element.24, pred[1024,2048]{0,1:T(8,128)(4,1)S(1)} %broadcast_compare_fusion, ...), kind=kOutput, calls=%fused_computation.8 | convolution fusion | flops 2264924160 | bytes 104169472 | tf_op jit(solution)/shard_map/qkgd,tkd->kgqt/dot_general | solution.py:86
  219.3 15.6 %fusion.27 = bf16[2048,1,64]{0,2,1:T(8,128)(2,1)} fusion(bf16[1024,8,64]{0,2,1:T(8,128)(2,1)S(1)} %copy-done.4, bf16[8,1024,2048]{1,2,0:T(8,128)(2,1)} %fusion.5), kind=kOutput, calls=%fused_computation.32 | convolution fusion | flops 2147745792 | bytes 34865152 | tf_op jit(solution)/shard_map/kgqt,qkgd->tkd/dot_general | solution.py:89
  238.1 3.3 all-to-all-start.7
  244.1 2.1 all-to-all-done.7
  246.2 3.3 all-to-all-start.6
  249.6 2.6 copy.63
  252.2 2.7 reshape.239
  254.9 4.4 all-to-all-start.3
  259.4 14.7 %fusion.40 = bf16[1024,8,64]{0,2,1:T(8,128)(2,1)} fusion(bf16[8,1024,2048]{1,2,0:T(8,128)(2,1)} %fusion.5, bf16[2048,1,64]{0,2,1:T(8,128)(2,1)S(1)} %copy-done.13), kind=kOutput, calls=%fused_computation.45 | convolution fusion | flops 2148532224 | bytes 34865152 | tf_op jit(solution)/shard_map/kgqt,tkd->qkgd/dot_general | solution.py:88
  274.0 2.6 copy.69
  276.7 2.7 reshape.241
  280.5 4.4 all-to-all-start.5
  285.8 2.0 fusion.61
  287.8 1.9 fusion.63
  289.7 4.3 reshape.240
  294.0 3.5 copy.89
  298.9 4.3 reshape.242
  303.2 3.8 copy.70
  309.0 8.7 %fusion.65 = f32[2048,2048]{1,0:T(8,128)} fusion(bf16[256,2048]{0,1:T(8,128)(2,1)S(1)} %bitcast.176, bf16[256,2048]{1,0:T(8,128)(2,1)S(1)} %copy-done.2, f32[2048]{0:T(1024)S(1)} %copy-done.23, f32[256]{0:T(256)S(1)} %copy-done.26), kind=kOutput, calls=%fused_computation.93 | convolution fusion | flops 2149580800 | bytes 18883584 | tf_op jit(solution)/shard_map/ta,tb->ab/dot_general | solution.py:102
  317.7 8.5 %fusion.75 = f32[2048,2048]{1,0:T(8,128)} fusion(bf16[256,2048]{0,1:T(8,128)(2,1)S(1)} %bitcast.171, bf16[256,2048]{1,0:T(8,128)(2,1)S(1)} %copy-done.6), kind=kOutput, calls=%fused_computation.97 | convolution fusion | flops 2147483648 | bytes 18874368 | tf_op jit(solution)/shard_map/ta,tb->ab/dot_general | solution.py:82
  326.2 6.2 fusion.74
  332.9 2.3 fusion.34
  335.2 24.7 %psum.39 = f32[2048]{0:T(1024)} all-reduce(f32[2048]{0:T(1024)S(1)} %get-tuple-element.7), channel_id=1, replica_groups=mesh['hp'=4,'cp'=2] {'hp','cp'}, use_global_device_ids=true, to_apply=%region_11.12 | all-reduce | flops 2048 | bytes 16384 | tf_op jit(solution)/shard_map/psum | solution.py:109
  359.9 3.6 fusion.33
  363.5 6.7 fusion.15
  370.2 391.8 %all-reduce.3.cloned.1.call-done = (f32[2048,2048]{1,0:T(8,128)}, f32[2048,256]{1,0:T(8,128)}, f32[2048,256]{1,0:T(8,128)}, f32[2048,2048]{1,0:T(8,128)}) async-done(((f32[2048,2048]{1,0:T(8,128)}, f32[2048,256]{1,0:T(8,128)}, f32[2048,256]{1,0:T(8,128)}, f32[2048,2048]{1,0:T(8,128)}), (f32[2048,2048]{1,0:T(8,128)}, f32[2048,256]{1,0:T(8,128)}, f32[2048,256]{1,0:T(8,128)}, ...) | async-done | bytes 37748752 | tf_op jit(solution)/shard_map/psum | solution.py:109
  761.9 14.1 %copy.103 = f32[2048,2048]{1,0:T(8,128)} copy(f32[2048,2048]{1,0:T(8,128)} %get-tuple-element.30) | data formatting | bytes 33554432
  780.9 6.2 copy.106
  (109 shorter events, 26.6 us)
Async XLA Ops:
  7.2 2.4 copy-start
  7.2 10.7 %copy-start.1 = (bf16[256,2048]{1,0:T(8,128)(2,1)S(1)}, bf16[256,2048]{1,0:T(8,128)(2,1)}, u32[]{:S(2)}) copy-start(bf16[256,2048]{1,0:T(8,128)(2,1)} %param.9) | copy-start | bytes 3145732
  7.2 10.6 %copy-start.27 = (s32[256]{0:T(256)S(1)}, s32[256]{0:T(256)}, u32[]{:S(2)}) copy-start(s32[256]{0:T(256)} %param.11) | copy-start | bytes 3076
  8.9 30.2 %copy-start.25 = (f32[256]{0:T(256)}, f32[256]{0:T(256)S(1)}, u32[]{:S(2)}) copy-start(f32[256]{0:T(256)S(1)} %add_rsqrt_fusion) | copy-start | bytes 3076
  9.6 29.5 %copy-start.22 = (f32[2048]{0:T(1024)}, f32[2048]{0:T(1024)S(1)}, u32[]{:S(2)}) copy-start(f32[2048]{0:T(1024)S(1)} %convert_element_type.107) | copy-start | bytes 24580
  12.1 7.6 copy-start.28
  12.1 13.8 %copy-start.5 = (bf16[256,2048]{1,0:T(8,128)(2,1)S(1)}, bf16[256,2048]{1,0:T(8,128)(2,1)}, u32[]{:S(2)}) copy-start(bf16[256,2048]{1,0:T(8,128)(2,1)} %param.10) | copy-start | bytes 3145732
  12.1 10.5 %all-to-all-start = ((bf16[256,4,64]{0,2,1:T(8,128)(2,1)}), bf16[256,4,64]{0,2,1:T(8,128)(2,1)S(1)}, u32[]{:S(2)}, u32[]{:S(2)}) async-start(bf16[256,4,64]{0,2,1:T(8,128)(2,1)} %bitcast.2), calls=%async_computation | async-start | bytes 262144 | tf_op jit(solution)/shard_map/all_to_all | solution.py:68
  19.9 26.0 %copy-start.16 = (f32[256,32]{0,1:T(8,128)}, f32[256,32]{0,1:T(8,128)S(1)}, u32[]{:S(2)}) copy-start(f32[256,32]{0,1:T(8,128)S(1)} %get-tuple-element.21) | copy-start | bytes 98308
  20.0 26.0 %copy-start.18 = (f32[256,32]{0,1:T(8,128)}, f32[256,32]{0,1:T(8,128)S(1)}, u32[]{:S(2)}) copy-start(f32[256,32]{0,1:T(8,128)S(1)} %get-tuple-element.22) | copy-start | bytes 98308
  22.6 12.3 %all-to-all-start.1 = ((bf16[256,4,64]{0,2,1:T(8,128)(2,1)}), bf16[256,4,64]{0,2,1:T(8,128)(2,1)S(1)}, u32[]{:S(2)}, u32[]{:S(2)}) async-start(bf16[256,4,64]{0,2,1:T(8,128)(2,1)} %pad_maximum_fusion.2), calls=%async_computation.1 | async-start | bytes 262144 | tf_op jit(solution)/shard_map/all_to_all | solution.py:67
  35.0 15.8 %all-to-all-start.4 = ((bf16[256,32,64]{0,2,1:T(8,128)(2,1)}), bf16[256,32,64]{0,2,1:T(8,128)(2,1)S(1)}, u32[]{:S(2)}, u32[]{:S(2)}) async-start(bf16[256,32,64]{0,2,1:T(8,128)(2,1)} %bitcast.180), calls=%async_computation.4 | async-start | bytes 2097152 | tf_op jit(solution)/shard_map/all_to_all | solution.py:84
  50.8 4.3 copy-start.8
  50.8 17.3 %all-to-all-start.2 = ((bf16[256,32,64]{0,2,1:T(8,128)(2,1)}), bf16[256,32,64]{0,2,1:T(8,128)(2,1)}, u32[]{:S(2)}, u32[]{:S(2)}) async-start(bf16[256,32,64]{0,2,1:T(8,128)(2,1)} %pad_maximum_fusion), calls=%async_computation.2 | async-start | bytes 2097152 | tf_op jit(solution)/shard_map/all_to_all | solution.py:66
  55.1 179.8 %reduce-scatter.5.cloned.1.call-start = ((), (), s32[]{:S(2)}) async-start(), calls=%async_computation.11 | async-start | bytes 393216 | tf_op jit(solution)/shard_map/reduce_scatter | solution.py:92
  55.2 5.9 copy-start.9
  61.0 12.6 %copy-start.12 = (bf16[2048,1,64]{0,2,1:T(8,128)(2,1)}, bf16[2048,1,64]{0,2,1:T(8,128)(2,1)S(1)}, u32[]{:S(2)}) copy-start(bf16[2048,1,64]{0,2,1:T(8,128)(2,1)S(1)} %all_gather.7) | copy-start | bytes 786436
  120.2 27.5 %copy-start.24 = (bf16[2048,1,64]{0,2,1:T(8,128)(2,1)S(1)}, bf16[2048,1,64]{0,2,1:T(8,128)(2,1)}, u32[]{:S(2)}) copy-start(bf16[2048,1,64]{0,2,1:T(8,128)(2,1)} %all_gather.6) | copy-start | bytes 786436
  147.5 94.0 %reduce-scatter.3.cloned.1.call-start = ((), (), s32[]{:S(2)}) async-start(), calls=%async_computation.10 | async-start | bytes 393216 | tf_op jit(solution)/shard_map/reduce_scatter | solution.py:91
  147.7 32.6 %copy-start.14 = (bf16[1024,8,64]{0,2,1:T(8,128)(2,1)S(1)}, bf16[1024,8,64]{0,2,1:T(8,128)(2,1)}, u32[]{:S(2)}) copy-start(bf16[1024,8,64]{0,2,1:T(8,128)(2,1)} %reshape.224) | copy-start | bytes 3145732
  180.3 39.0 %copy-start.4 = (bf16[1024,8,64]{0,2,1:T(8,128)(2,1)S(1)}, bf16[1024,8,64]{0,2,1:T(8,128)(2,1)}, u32[]{:S(2)}) copy-start(bf16[1024,8,64]{0,2,1:T(8,128)(2,1)} %reshape.219) | copy-start | bytes 3145732
  238.1 8.1 %all-to-all-start.7 = ((bf16[4,2,8192]{2,1,0:T(2,128)(2,1)}), bf16[4,2,8192]{2,1,0:T(2,128)(2,1)S(1)}, u32[]{:S(2)}, u32[]{:S(2)}) async-start(bf16[4,2,8192]{2,1,0:T(2,128)(2,1)} %reshape.245), calls=%async_computation.9 | async-start | bytes 262144 | tf_op jit(solution)/shard_map/all_to_all | solution.py:95
  246.2 3.3 copy-start.20
  246.2 8.7 %all-to-all-start.6 = ((bf16[4,2,8192]{2,1,0:T(2,128)(2,1)}), bf16[4,2,8192]{2,1,0:T(2,128)(2,1)S(1)}, u32[]{:S(2)}, u32[]{:S(2)}) async-start(bf16[4,2,8192]{2,1,0:T(2,128)(2,1)} %reshape.243), calls=%async_computation.7 | async-start | bytes 262144 | tf_op jit(solution)/shard_map/all_to_all | solution.py:94
  252.2 7.1 copy-start.13
  254.9 25.6 %all-to-all-start.3 = ((bf16[4,2,65536]{2,1,0:T(2,128)(2,1)}), bf16[4,2,65536]{2,1,0:T(2,128)(2,1)}, u32[]{:S(2)}, u32[]{:S(2)}) async-start(bf16[4,2,65536]{2,1,0:T(2,128)(2,1)} %reshape.239), calls=%async_computation.3 | async-start | bytes 2097152 | tf_op jit(solution)/shard_map/all_to_all | solution.py:80
  279.6 5.3 copy-start.17
  279.6 5.3 copy-start.19
  279.7 5.3 copy-start.21
  280.4 5.4 copy-start.2
  280.4 5.4 copy-start.23
  280.4 5.4 copy-start.26
  280.5 18.5 %all-to-all-start.5 = ((bf16[4,2,65536]{2,1,0:T(2,128)(2,1)}), bf16[4,2,65536]{2,1,0:T(2,128)(2,1)}, u32[]{:S(2)}, u32[]{:S(2)}) async-start(bf16[4,2,65536]{2,1,0:T(2,128)(2,1)} %reshape.241), calls=%async_computation.5 | async-start | bytes 2097152 | tf_op jit(solution)/shard_map/all_to_all | solution.py:93
  284.9 477.1 %all-reduce.3.cloned.1.call-start = ((), (), s32[]{:S(2)}) async-start(), calls=%async_computation.12 | async-start | bytes 75497472 | tf_op jit(solution)/shard_map/psum | solution.py:109
  309.0 8.7 %copy-start.7 = (bf16[256,32,64]{0,2,1:T(8,128)(2,1)}, bf16[256,32,64]{0,2,1:T(8,128)(2,1)S(1)}, u32[]{:S(2)}) copy-start(bf16[256,32,64]{0,2,1:T(8,128)(2,1)S(1)} %pad_maximum_fusion.1) | copy-start | bytes 3145732
  309.0 8.7 %copy-start.6 = (bf16[256,2048]{1,0:T(8,128)(2,1)S(1)}, bf16[256,2048]{1,0:T(8,128)(2,1)}, u32[]{:S(2)}) copy-start(bf16[256,2048]{1,0:T(8,128)(2,1)} %param.10) | copy-start | bytes 3145732
  326.2 6.2 copy-start.15
  761.9 14.1 %copy-start.11 = (f32[2048,256]{1,0:T(8,128)S(1)}, f32[2048,256]{1,0:T(8,128)}, u32[]{:S(2)}) copy-start(f32[2048,256]{1,0:T(8,128)} %get-tuple-element.31) | copy-start | bytes 6291460
  761.9 19.0 %copy-start.3 = (f32[2048,2048]{1,0:T(8,128)S(1)}, f32[2048,2048]{1,0:T(8,128)}, u32[]{:S(2)}) copy-start(f32[2048,2048]{1,0:T(8,128)} %get-tuple-element.33) | copy-start | bytes 50331652
  776.1 3.1 copy-start.10
Sparse Core Ops, SparseCore 0:
  147.6 5.1 reduce-scatter.4
  235.0 5.1 reduce-scatter.2
  326.3 435.5 all-reduce.2
where the time goes:
time: 803 us; the launch traced here: 794 us
  waiting for transfers between devices  402 us (50%)
  matrix products  209 us (26%)
  local copies, waits for them, and re-layouts  69.2 us (9%)
  other arithmetic  36.8 us (5%)
  starting transfers between devices  33.2 us (4%)
  blocking collectives  29.1 us (4%)
  between operations  14.9 us (2%)
    psum x1, waiting for transfers between devices, device_step(): lax.psum((grad_wq, grad_wk, grad_wv, grad_wo, grad_gain), ('hp', 'cp'))  392 us
    unnamed x72, local copies, waits for them, and re-layouts  41.9 us
    dot_general x1, matrix products, device_step(): jnp.einsum('qkgd,tkd->kgqt', do_head, v_all, preferred_element_type=jnp.f...  38.9 us
    dot_general x1, matrix products, device_step(): jnp.einsum('kgqt,tkd->qkgd', prob_b16, v_all, preferred_element_type=jnp....  32.6 us
    dot_general x1, matrix products, device_step(): jnp.einsum('kgqt,qkgd->tkd', prob_b16, do_head, preferred_element_type=jn...  27.3 us
    dot_general x1, matrix products, device_step(): jnp.einsum('qkgd,tkd->kgqt', q_head, k_all, preferred_element_type=jnp.fl...  25 us
    psum x1, blocking collectives, device_step(): lax.psum((grad_wq, grad_wk, grad_wv, grad_wo, grad_gain), ('hp', 'cp'))  24.7 us
    reduce_sum x1, other arithmetic, device_step(): prob_f32 = prob_f32 / jnp.sum(prob_f32, axis=-1, keepdims=True)  21.5 us
  transfers between devices with their start and end apart: 11, of which 5 were waited for; matrix products, arithmetic and copies ran while one was open for 22% of the time, Pallas kernels for 0%

commit v1 on v0

v1 whole, which is shorter than its diff:
```python
import functools
import math

import jax
import jax.numpy as jnp
from jax import lax
from jax.experimental import pallas as pl
from jax.experimental.pallas import tpu as pltpu
from jax.sharding import PartitionSpec as P

NORM_EPS = 1e-5
BLK = 256
HEADS = 4
DH = 64
NB = 8
CW = HEADS * BLK
EXP2_SCALE = (DH ** -0.5) * math.log2(math.e)
F32 = jnp.float32
BF16 = jnp.bfloat16


def seq_block(d):
    cp, half, sub = d // 4, (d // 2) % 2, d % 2
    return 2 * ((1 - half) * cp + half * (3 - cp)) + sub


def stored_block(j):
    b, sub = j // 2, j % 2
    half = b // 2
    cp = (1 - half) * b + half * (3 - b)
    return cp * 4 + half * 2 + sub


def nt_dot(a, b):
    return lax.dot_general(a, b, (((1,), (1,)), ((), ())), preferred_element_type=F32)


def dot(a, b):
    return jnp.dot(a, b, preferred_element_type=F32)


def rope_pairs(t, cos_t, sin_t):
    lane = lax.broadcasted_iota(jnp.int32, t.shape, 1)
    partner = jnp.where(lane % DH < DH // 2, pltpu.roll(t, 128 - DH // 2, 1), pltpu.roll(t, DH // 2, 1))
    return t * cos_t + partner * sin_t


def rows_of(b):
    return pl.ds(pl.multiple_of(b * BLK, BLK), BLK)


def causal_tile():
    row = lax.broadcasted_iota(jnp.int32, (BLK, CW), 0)
    col = lax.broadcasted_iota(jnp.int32, (BLK, CW), 1)
    return row <= col % BLK


def project_block(d, x, gain, w_ref, cos_ref, sin_ref, ht_ref, q_ref, k_ref, v_ref):
    xf = x.astype(F32)
    inv = lax.rsqrt(jnp.mean(xf * xf, axis=-1, keepdims=True) + NORM_EPS)
    h = (xf * inv * gain).astype(BF16)
    ht_ref[:, rows_of(d)] = h.T
    y = dot(h, w_ref[...])
    dst = rows_of(seq_block(d))
    cos_t, sin_t = cos_ref[rows_of(d), :], sin_ref[rows_of(d), :]
    for p in range(HEADS // 2):
        qr = rope_pairs(y[:, 128 * p:128 * (p + 1)], cos_t, sin_t).astype(BF16)
        q_ref[2 * p, dst, :] = qr[:, :DH]
        q_ref[2 * p + 1, dst, :] = qr[:, DH:]
    kv = y[:, 128 * (HEADS // 2):]
    k_ref[dst, :] = rope_pairs(kv, cos_t, sin_t).astype(BF16)[:, :DH]
    v_ref[dst, :] = kv.astype(BF16)[:, DH:]


def attend_block(j, q_ref, k_ref, vt_ref, e_ref, m_ref, ot_ref, lse_ref):
    q4 = q_ref[:, rows_of(j), :].reshape(CW, DH)

    def score_tile(kb, carry, masked):
        m_old, l_old = carry
        s = nt_dot(k_ref[rows_of(kb), :], q4) * EXP2_SCALE
        if masked:
            s = jnp.where(causal_tile(), s, -1e30)
        m_new = jnp.maximum(m_old, jnp.max(s, axis=0, keepdims=True))
        e = jnp.exp2(s - m_new)
        e_ref[rows_of(kb), :] = e
        m_ref[pl.ds(kb, 1), :] = m_new
        return m_new, l_old * jnp.exp2(m_old - m_new) + jnp.sum(e, axis=0, keepdims=True)

    carry = (jnp.full((1, CW), -1e30, F32), jnp.zeros((1, CW), F32))
    carry = score_tile(j, carry, True)
    m_fin, l_fin = lax.fori_loop(0, j, functools.partial(score_tile, masked=False), carry)
    inv_l = 1.0 / l_fin
    lse = m_fin + jnp.log2(l_fin)

    def out_tile(kb, acc):
        f = jnp.exp2(m_ref[pl.ds(kb, 1), :] - m_fin) * inv_l
        p = (e_ref[rows_of(kb), :] * f).astype(BF16)
        return acc + dot(vt_ref[:, rows_of(kb)], p)

    acc = lax.fori_loop(0, j + 1, out_tile, jnp.zeros((DH, CW), F32)).astype(BF16)
    dst = rows_of(stored_block(j))
    for h in range(HEADS):
        ot_ref[DH * h:DH * (h + 1), dst] = acc[:, BLK * h:BLK * (h + 1)]
        lse_ref[h:h + 1, rows_of(j)] = lse[:, BLK * h:BLK * (h + 1)]


def forward_kernel(x_ref, gain_ref, w_ref, cos_ref, sin_ref, ht_ref, q_ref, k_ref, v_ref, ot_ref, lse_ref, e_ref, m_ref, vt_ref):
    def project(d, _):
        project_block(d, x_ref[rows_of(d), :], gain_ref[...], w_ref, cos_ref, sin_ref, ht_ref, q_ref, k_ref, v_ref)
        return 0

    lax.fori_loop(0, NB, project, 0)
    vt_ref[...] = v_ref[...].T

    def attend(j, _):
        attend_block(j, q_ref, k_ref, vt_ref, e_ref, m_ref, ot_ref, lse_ref)
        return 0

    lax.fori_loop(0, NB, attend, 0)


def backward_kernel(dy_ref, wo_ref, q_ref, k_ref, v_ref, ot_ref, lse_ref, cos_ref, sin_ref, gq_ref, dk_ref, dv_ref, do_ref, kt_ref):
    def project(d, _):
        do = nt_dot(dy_ref[rows_of(d), :], wo_ref[...]).astype(BF16)
        dst = rows_of(seq_block(d))
        for h in range(HEADS):
            do_ref[h, dst, :] = do[:, DH * h:DH * (h + 1)]
        return 0

    lax.fori_loop(0, NB, project, 0)
    kt_ref[...] = k_ref[...].T
    dk_ref[...] = jnp.zeros_like(dk_ref)
    dv_ref[...] = jnp.zeros_like(dv_ref)

    def attend(j, _):
        src = rows_of(stored_block(j))
        q4 = q_ref[:, rows_of(j), :].reshape(CW, DH)
        do4 = do_ref[:, rows_of(j), :].reshape(CW, DH)
        o4t = jnp.concatenate([ot_ref[DH * h:DH * (h + 1), src] for h in range(HEADS)], axis=1)
        lse = jnp.concatenate([lse_ref[h:h + 1, rows_of(j)] for h in range(HEADS)], axis=1)
        delta = jnp.sum(do4.astype(F32).T * o4t.astype(F32), axis=0, keepdims=True)

        def tile(kb, dqt, masked):
            keys = rows_of(kb)
            p = jnp.exp2(nt_dot(k_ref[keys, :], q4) * EXP2_SCALE - lse)
            if masked:
                p = jnp.where(causal_tile(), p, 0.0)
            dp = nt_dot(v_ref[keys, :], do4)
            dv_ref[keys, :] += dot(p.astype(BF16), do4)
            ds = (p * (dp - delta)).astype(BF16)
            dk_ref[keys, :] += dot(ds, q4)
            return dqt + dot(kt_ref[:, keys], ds)

        dqt = tile(j, jnp.zeros((DH, CW), F32), True)
        dqt = lax.fori_loop(0, j, functools.partial(tile, masked=False), dqt) * (DH ** -0.5)
        cos_t, sin_t = cos_ref[src, :], sin_ref[src, :]
        for p in range(HEADS // 2):
            pair = jnp.concatenate([dqt[:, BLK * (2 * p):BLK * (2 * p + 1)], dqt[:, BLK * (2 * p + 1):BLK * (2 * p + 2)]], axis=0)
            dq = pair.T.astype(BF16).astype(F32)
            gq_ref[src, 128 * p:128 * (p + 1)] = rope_pairs(dq, cos_t, -sin_t).astype(BF16)
        return 0

    lax.fori_loop(0, NB, attend, 0)


VMEM_SPEC = pl.BlockSpec(memory_space=pltpu.VMEM)


def run_forward(x_all, gain, w_qkv, cos_t, sin_t):
    toks, width = x_all.shape
    return pl.pallas_call(
        forward_kernel,
        out_shape=(
            jax.ShapeDtypeStruct((width, toks), BF16),
            jax.ShapeDtypeStruct((HEADS, toks, DH), BF16),
            jax.ShapeDtypeStruct((toks, DH), BF16),
            jax.ShapeDtypeStruct((toks, DH), BF16),
            jax.ShapeDtypeStruct((HEADS * DH, toks), BF16),
            jax.ShapeDtypeStruct((HEADS, toks), F32),
        ),
        in_specs=[VMEM_SPEC] * 5,
        out_specs=(VMEM_SPEC,) * 6,
        scratch_shapes=[pltpu.VMEM((toks, CW), F32), pltpu.VMEM((NB, CW), F32), pltpu.VMEM((DH, toks), BF16)],
        compiler_params=pltpu.CompilerParams(vmem_limit_bytes=60 * 1024 * 1024),
        cost_estimate=pl.CostEstimate(flops=30_000_000_000, bytes_accessed=20_000_000, transcendentals=0),
        name="attn_forward",
    )(x_all, gain, w_qkv, cos_t, sin_t)


def run_backward(dy_all, w_o, q, k, v, o_t, lse, cos_t, sin_t):
    toks = dy_all.shape[0]
    return pl.pallas_call(
        backward_kernel,
        out_shape=(
            jax.ShapeDtypeStruct((toks, HEADS * DH), BF16),
            jax.ShapeDtypeStruct((toks, DH), F32),
            jax.ShapeDtypeStruct((toks, DH), F32),
        ),
        in_specs=[VMEM_SPEC] * 9,
        out_specs=(VMEM_SPEC,) * 3,
        scratch_shapes=[pltpu.VMEM((HEADS, toks, DH), BF16), pltpu.VMEM((DH, toks), BF16)],
        compiler_params=pltpu.CompilerParams(vmem_limit_bytes=60 * 1024 * 1024),
        cost_estimate=pl.CostEstimate(flops=40_000_000_000, bytes_accessed=20_000_000, transcendentals=0),
        name="attn_backward",
    )(dy_all, w_o, q, k, v, o_t, lse, cos_t, sin_t)


def seq_to_stored(a):
    return jnp.concatenate([a[0:512], a[1536:2048], a[512:1536]], axis=0)


def rope_undo(vectors, cos_t, sin_t):
    half_dim = vectors.shape[-1] // 2
    lo_half = vectors[..., :half_dim]
    hi_half = vectors[..., half_dim:]
    return jnp.concatenate([lo_half * cos_t + hi_half * sin_t, hi_half * cos_t - lo_half * sin_t], axis=-1)


def solution(mesh):
    def device_step(hidden, grad_out, positions, norm_gain, w_q, w_k, w_v, w_o, inv_freq):
        rows = hidden.shape[0]
        hp, cp = lax.axis_index('hp'), lax.axis_index('cp')
        me_tok, me_head = cp * 4 + hp, hp * 2 + cp
        x_all = lax.all_gather(hidden, ('cp', 'hp'), axis=0, tiled=True)
        dy_all = lax.all_gather(grad_out, ('cp', 'hp'), axis=0, tiled=True)
        pos_all = lax.all_gather(positions, ('cp', 'hp'), axis=0, tiled=True)
        angles = pos_all.astype(F32)[:, None] * inv_freq[None, :]
        cos_h, sin_h = jnp.cos(angles), jnp.sin(angles)
        cos_t = jnp.concatenate([cos_h] * 4, axis=1)
        sin_t = jnp.concatenate([-sin_h, sin_h] * 2, axis=1)
        gain = norm_gain.astype(F32)[None, :]
        hw = HEADS * DH
        w_qkv = jnp.concatenate([
            lax.dynamic_slice_in_dim(w_q, me_head * hw, hw, 1),
            lax.dynamic_slice_in_dim(w_k, hp * DH, DH, 1),
            lax.dynamic_slice_in_dim(w_v, hp * DH, DH, 1)], axis=1)
        wo_my = lax.dynamic_slice_in_dim(w_o, me_head * hw, hw, 0)
        h_t, q, k, v, o_t, lse = run_forward(x_all, gain, w_qkv, cos_t, sin_t)
        ot_all = lax.all_gather(o_t, ('hp', 'cp'), axis=0, tiled=True)
        g_q, dk_part, dv_part = run_backward(dy_all, wo_my, q, k, v, o_t, lse, cos_t, sin_t)
        gq_all = lax.all_gather(g_q, ('hp', 'cp'), axis=0)
        part = seq_to_stored(jnp.concatenate([dk_part * (DH ** -0.5), dv_part], axis=1)).astype(BF16)
        pair = lax.all_gather(part, 'cp', axis=0).astype(F32)
        dkv = (pair[0] + pair[1]).astype(BF16)
        g_k = rope_undo(dkv[:, :DH].astype(F32), cos_h, sin_h).astype(BF16)
        gkv_all = lax.all_gather(jnp.concatenate([g_k, dkv[:, DH:]], axis=1), 'hp', axis=0)
        x_f32 = hidden.astype(F32)
        inv_rms = lax.rsqrt(jnp.mean(x_f32 * x_f32, axis=-1, keepdims=True) + NORM_EPS)
        x_hat = x_f32 * inv_rms
        o_mine = lax.dynamic_slice_in_dim(ot_all, me_tok * rows, rows, 1)
        output = (x_f32 + jnp.einsum('at,ab->tb', o_mine, w_o, preferred_element_type=F32)).astype(BF16)
        grad_wo = jnp.dot(ot_all, dy_all, preferred_element_type=F32)
        gq_cols = gq_all.transpose(1, 0, 2).reshape(NB * rows, NB * hw)
        gk_cols = gkv_all[:, :, :DH].transpose(1, 0, 2).reshape(NB * rows, 4 * DH)
        gv_cols = gkv_all[:, :, DH:].transpose(1, 0, 2).reshape(NB * rows, 4 * DH)
        grad_wq = jnp.dot(h_t, gq_cols, preferred_element_type=F32)
        grad_wk = jnp.dot(h_t, gk_cols, preferred_element_type=F32)
        grad_wv = jnp.dot(h_t, gv_cols, preferred_element_type=F32)
        mine = lambda a: lax.dynamic_slice_in_dim(a, me_tok * rows, rows, 0)
        d_norm = (jnp.einsum('tb,ab->ta', mine(gq_cols), w_q, preferred_element_type=F32)
                  + jnp.einsum('tb,ab->ta', mine(gk_cols), w_k, preferred_element_type=F32)
                  + jnp.einsum('tb,ab->ta', mine(gv_cols), w_v, preferred_element_type=F32))
        gain_part = jnp.sum(d_norm * x_hat, axis=0, keepdims=True)
        grad_gain = jnp.sum(lax.all_gather(gain_part, ('cp', 'hp'), axis=0, tiled=True), axis=0)
        d_hat = d_norm * gain
        grad_hidden = (grad_out.astype(F32) + inv_rms * (d_hat - x_hat * jnp.mean(d_hat * x_hat, axis=-1, keepdims=True))).astype(BF16)
        return output, grad_hidden, grad_wq, grad_wk, grad_wv, grad_wo, grad_gain

    seq_spec = P(('cp', 'hp'), None)
    whole = P()
    return jax.shard_map(device_step, mesh=mesh, in_specs=(seq_spec, seq_spec, P(('cp', 'hp')), whole, whole, whole, whole, whole, whole), out_specs=(seq_spec, seq_spec, whole, whole, whole, whole, whole), check_vma=False)
```

time: 803 us -> 349 us (0.43); the launches traced: 794 us -> 349 us
  waiting for transfers between devices: 402 us -> 94.2 us
  matrix products: 209 us -> 76.6 us
  Pallas kernels: 0 us -> 89.4 us
  local copies, waits for them, and re-layouts: 69.2 us -> 25.1 us
  starting transfers between devices: 33.2 us -> 0.42 us
  other arithmetic: 36.8 us -> 22.9 us
    psum x1 -> x0, waiting for transfers between devices: 392 us -> none  [device_step(): lax.psum((grad_wq, grad_wk, grad_wv, grad_wo, grad_gain), ('hp', 'cp'))]
    dot_general x18 -> x8, matrix products: 209 us -> 76.6 us  [the longest x1 24.3 us: device_step(): grad_wq = jnp.dot(h_t, gq_cols, preferred_element_type=F32)]
    all_gather x0 -> x6, waiting for transfers between devices: none -> 91.8 us  [the longest x1 29.2 us: device_step(): lax.all_gather(jnp.concatenate([g_k, dkv[:, DH:]], axis=1), 'hp', axis=0)]
    pallas_call x0 -> x2, Pallas kernels: none -> 89.4 us  [the longest x1 46.3 us: run_forward(): pl.pallas_call(forward_kernel, out_shape=(jax.ShapeDtypeStruct((width, to...]
    unnamed x72 -> x26, local copies, waits for them, and re-layouts: 41.9 us -> 5.21 us
    all_to_all x8 -> x0, starting transfers between devices: 32.9 us -> none  [the longest x1 5.7 us: device_step(): v_head = lax.all_to_all(v_val, 'hp', 1, 0, tiled=True)]
    psum x1 -> x0, blocking collectives: 24.7 us -> none  [device_step(): lax.psum((grad_wq, grad_wk, grad_wv, grad_wo, grad_gain), ('hp', 'cp'))]
    all_gather x2, blocking collectives: 4.45 us -> 25.7 us  [the longest x1 13.6 us: device_step(): pos_all = lax.all_gather(positions, ('cp', 'hp'), axis=0, tiled=True)]
  transfers between devices with their start and end apart: 11 -> 6, of which waited for: 5 -> 5; matrix products, arithmetic and copies ran while one was open for 22% -> 24% of each run, Pallas kernels for 0% -> 13%
where the time goes in v1:
time: 349 us
  waiting for transfers between devices  94.2 us (27%)
  Pallas kernels  89.4 us (26%)
  matrix products  76.6 us (22%)
  blocking collectives  25.7 us (7%)
  local copies, waits for them, and re-layouts  25.1 us (7%)
  other arithmetic  22.9 us (7%)
  between operations  14.3 us (4%)
    pallas_call x1, Pallas kernels, run_forward(): pl.pallas_call(forward_kernel, out_shape=(jax.ShapeDtypeStruct((width, to...  46.3 us
    pallas_call x1, Pallas kernels, run_backward(): pl.pallas_call(backward_kernel, out_shape=(jax.ShapeDtypeStruct((toks, HE...  43.1 us
    all_gather x1, waiting for transfers between devices, device_step(): lax.all_gather(jnp.concatenate([g_k, dkv[:, DH:]], axis=1), 'hp', axis=0)  29.2 us
    all_gather x1, waiting for transfers between devices, device_step(): gq_all = lax.all_gather(g_q, ('hp', 'cp'), axis=0)  26.9 us
    all_gather x1, waiting for transfers between devices, device_step(): x_all = lax.all_gather(hidden, ('cp', 'hp'), axis=0, tiled=True)  25.7 us
    dot_general x1, matrix products, device_step(): grad_wq = jnp.dot(h_t, gq_cols, preferred_element_type=F32)  24.3 us
    dot_general x1, matrix products, device_step(): grad_wo = jnp.dot(ot_all, dy_all, preferred_element_type=F32)  21.9 us
    all_gather x1, blocking collectives, device_step(): pos_all = lax.all_gather(positions, ('cp', 'hp'), axis=0, tiled=True)  13.6 us
  transfers between devices with their start and end apart: 6, of which 5 were waited for; matrix products, arithmetic and copies ran while one was open for 24% of the time, Pallas kernels for 13%

profile of v1, /device:TPU:0, one launch (start us, length us, event | category | flops | bytes accessed | tf_op | source)
XLA Modules:
  0.0 348.6 jit_solution(12844773516383352279)
XLA Ops:
  7.2 0.7 all-gather.11.cloned.1.call-update
  8.0 0.7 all-gather.15.cloned.1.call-update
  8.7 0.6 convert_element_type.40
  9.3 13.6 %all-gather.3 = s32[8,1,256]{2,1,0:T(1,128)S(1)} all-gather(s32[1,1,256]{2,1,0:T(1,128)S(1)} %bitcast.45), channel_id=1, replica_groups=mesh['hp'=4,'cp'=2] {'cp','hp'}, dimensions={0}, use_global_device_ids=true | all-gather | bytes 9216 | tf_op jit(solution)/shard_map/all_gather | solution.py:226
  23.0 1.4 constant_dynamic-slice_fusion.3
  24.5 2.3 constant_dynamic-slice_fusion.wo_ref
  26.8 0.4 constant_dynamic-slice_fusion.1
  27.2 1.5 pad_maximum_fusion.w_ref
  28.6 3.7 %fusion.13 = (f32[2048,32]{1,0:T(8,128)S(1)}, f32[2048,32]{1,0:T(8,128)S(1)}, f32[2048,32]{1,0:T(8,128)S(1)}) fusion(f32[2048]{0:T(1024)S(1)} %bitcast.43, f32[32]{0:T(128)S(1)} %copy-done.10), kind=kLoop, calls=%fused_computation.21 | loop fusion | flops 131072 | bytes 794752 | tf_op jit(solution)/shard_map/neg | solution.py:230
  32.3 3.0 pad_maximum_fusion.1
  35.4 25.7 %all-gather.11.cloned.1.call-done.x_ref = bf16[2048,2048]{1,0:T(8,128)(2,1)} async-done(((bf16[256,2048]{1,0:T(8,128)(2,1)}), bf16[2048,2048]{1,0:T(8,128)(2,1)}) %all-gather.11.cloned.1.call-update) | async-done | bytes 8388624 | tf_op jit(solution)/shard_map/all_gather | solution.py:224
  61.0 46.3 %attn_forward.1 = (bf16[2048,2048]{1,0:T(8,128)(2,1)}, bf16[4,2048,64]{2,1,0:T(8,128)(2,1)}, bf16[2048,64]{1,0:T(8,128)(2,1)}, bf16[2048,64]{1,0:T(8,128)(2,1)},...) custom-call(bf16[2048,2048]{1,0:T(8,128)(2,1)} %all-gather.11.cloned.1.call-done.x_ref, f32[1,2048]{1,0:T(1,128)} %bitcast.42, ...), custom_call_target="tpu_custom_call" | custom-call | flops 30000001024 | bytes 20000000 | tf_op jit(solution)/shard_map/attn_forward/pallas_call | solution.py:171
  107.3 3.9 %all-gather.15.cloned.1.call-done.dy_ref = bf16[2048,2048]{1,0:T(8,128)(2,1)} async-done(((bf16[256,2048]{1,0:T(8,128)(2,1)}), bf16[2048,2048]{1,0:T(8,128)(2,1)}) %all-gather.15.cloned.1.call-update) | async-done | bytes 8388624 | tf_op jit(solution)/shard_map/all_gather | solution.py:225
  111.2 43.1 %attn_backward.1 = (bf16[2048,256]{1,0:T(8,128)(2,1)}, f32[2048,64]{1,0:T(8,128)}, f32[2048,64]{1,0:T(8,128)}) custom-call(bf16[2048,2048]{1,0:T(8,128)(2,1)} %all-gather.15.cloned.1.call-done.dy_ref, bf16[256,2048]{1,0:T(8,128)(2,1)} %constant_dynamic-slice_fusion.wo_ref, bf16[4,2048,64]{2,1,0:T(8,128)(2,1)} %get-tuple-element.17.q_ref, ...), custom_call_target="tpu_custom_call" | custom-call | flops 40000000000 | bytes 20000000 | tf_op jit(solution)/shard_map/attn_backward/pallas_call | solution.py:192
  154.3 1.4 broadcast_multiply_fusion
  155.7 0.2 copy-done.1
  155.9 0.1 fusion.24
  156.0 0.1 fusion.25
  156.2 0.8 pad_maximum_fusion.4
  157.0 0.2 all-gather.21.cloned.1.call-start
  157.3 6.0 %all-gather.17.cloned.1.call-done = bf16[2,2048,128]{2,1,0:T(8,128)(2,1)} async-done(((bf16[1,2048,128]{2,1,0:T(8,128)(2,1)}), bf16[2,2048,128]{2,1,0:T(8,128)(2,1)}) %all-gather.17.cloned.1.call-update) | async-done | bytes 1048592 | tf_op jit(solution)/shard_map/all_gather | solution.py:243
  163.3 1.4 convert_element_type.44
  164.6 0.1 fusion.22
  164.8 0.2 slice_convert_fusion
  165.0 4.8 %fusion.15 = (bf16[2048,32]{1,0:T(8,128)(2,1)S(1)}, bf16[2048,32]{1,0:T(8,128)(2,1)S(1)}) fusion(f32[2048,64]{1,0:T(8,128)S(1)} %get-tuple-element.33, f32[2048]{0:T(1024)S(1)} %bitcast.44, f32[32]{0:T(128)S(1)} %copy-done.10), kind=kLoop, calls=%fused_computation.23 | loop fusion | flops 589824 | bytes 794752 | tf_op jit(solution)/shard_map/convert
  169.8 1.3 pad_maximum_fusion.5
  171.1 0.0 all-gather.19.cloned.1.call-start
  171.2 0.5 all-gather.19.cloned.1.call-update
  171.8 0.5 all-gather.13.cloned.1.call-update
  172.3 0.3 fusion.10
  172.6 29.2 %all-gather.21.cloned.1.call-done = bf16[8192,128]{1,0:T(8,128)(2,1)} async-done(((bf16[2048,128]{1,0:T(8,128)(2,1)}), bf16[8192,128]{1,0:T(8,128)(2,1)}) %all-gather.21.cloned.1.call-update) | async-done | bytes 2097168 | tf_op jit(solution)/shard_map/all_gather | solution.py:246
  201.8 4.3 %fusion.33 = (bf16[4,2048,64]{2,1,0:T(8,128)(2,1)}, bf16[4,2048,64]{2,1,0:T(8,128)(2,1)S(1)}) fusion(bf16[4,2048,128]{2,1,0:T(8,128)(2,1)} %bitcast.37), kind=kLoop, calls=%fused_computation.57 | loop fusion | bytes 4194304 | tf_op jit(solution)/shard_map/slice | solution.py:255
  206.1 2.7 copy.30
  208.8 1.6 copy.29
  210.4 7.4 %fusion.36 = f32[2048,256]{1,0:T(8,128)} fusion(bf16[2048,2048]{1,0:T(8,128)(2,1)} %get-tuple-element.24, bf16[2048,256]{0,1:T(8,128)(2,1)} %bitcast.38), kind=kOutput, calls=%fused_computation.60 | convolution fusion | flops 2147483648 | bytes 11534336 | tf_op jit(solution)/shard_map/dot_general | solution.py:258
  217.8 7.1 %fusion.35 = f32[2048,256]{1,0:T(8,128)} fusion(bf16[2048,2048]{1,0:T(8,128)(2,1)} %get-tuple-element.24, bf16[2048,256]{0,1:T(8,128)(2,1)S(1)} %bitcast.40), kind=kOutput, calls=%fused_computation.59 | convolution fusion | flops 2147483648 | bytes 11534336 | tf_op jit(solution)/shard_map/dot_general | solution.py:257
  224.9 26.9 %all-gather.19.cloned.1.call-done = bf16[16384,256]{1,0:T(8,128)(2,1)} async-done(((bf16[2048,256]{1,0:T(8,128)(2,1)}), bf16[16384,256]{1,0:T(8,128)(2,1)}) %all-gather.19.cloned.1.call-update) | async-done | bytes 8388624 | tf_op jit(solution)/shard_map/all_gather | solution.py:241
  251.8 11.4 %copy.26 = bf16[8,2048,256]{1,2,0:T(8,128)(2,1)} copy(bf16[8,2048,256]{2,1,0:T(8,128)(2,1)} %bitcast.34) | data formatting | bytes 16777216 | tf_op jit(solution)/shard_map/all_gather | solution.py:241
  263.3 6.2 %fusion.19 = f32[256,2048]{1,0:T(8,128)S(1)} fusion(bf16[2048,2048]{1,0:T(8,128)(2,1)} %param.13, bf16[2048,2048]{0,1:T(8,128)(2,1)} %bitcast.35, s32[]{:T(128)S(6)} %select_n.16), kind=kOutput, calls=%fused_computation.30 | convolution fusion | flops 2147483648 | bytes 11534340 | tf_op jit(solution)/shard_map/tb,ab->ta/dot_general | solution.py:260
  269.5 0.5 convolution_add_fusion.1
  270.0 0.7 copy-done.3
  270.7 2.0 fusion.9
  272.7 12.1 %all-gather.2 = f32[16384]{0:T(1024)S(1)} all-gather(f32[2048]{0:T(1024)S(1)} %get-tuple-element.25), channel_id=4, replica_groups=mesh['hp'=4,'cp'=2] {'cp','hp'}, dimensions={0}, use_global_device_ids=true | all-gather | bytes 73728 | tf_op jit(solution)/shard_map/all_gather | solution.py:264
  284.8 0.6 reduce_sum.39
  285.4 2.9 fusion.8
  288.3 24.3 %fusion.34 = f32[2048,2048]{1,0:T(8,128)} fusion(bf16[2048,2048]{1,0:T(8,128)(2,1)} %get-tuple-element.24, bf16[2048,2048]{0,1:T(8,128)(2,1)} %bitcast.36), kind=kOutput, calls=%fused_computation.58 | convolution fusion | flops 17179869184 | bytes 33554432 | tf_op jit(solution)/shard_map/dot_general | solution.py:256
  312.6 7.2 %fusion.3 = bf16[256,2048]{1,0:T(8,128)(2,1)} fusion(bf16[2048,2048]{1,0:T(8,128)(2,1)} %param.16, bf16[256,2048]{1,0:T(8,128)(2,1)S(1)} %copy-done, bf16[2048,2048]{1,0:T(8,128)(2,1)} %all-gather.13.cloned.1.call-done, s32[]{:T(128)S(6)} %select_n.16), kind=kOutput, calls=%fused_computation.8 | convolution fusion | flops 2149056512 | bytes 11534340 | tf_op jit(solution)/shard_map/at,ab->tb/dot_general | solution.py:251
  319.8 21.9 %fusion.37 = f32[2048,2048]{1,0:T(8,128)} fusion(bf16[2048,2048]{1,0:T(8,128)(2,1)S(1)} %copy-done.7, bf16[2048,2048]{1,0:T(8,128)(2,1)} %all-gather.15.cloned.1.call-done.dy_ref), kind=kOutput, calls=%fused_computation.61 | convolution fusion | flops 17179869184 | bytes 33554432 | tf_op jit(solution)/shard_map/dot_general | solution.py:252
  (33 shorter events, 0.3 us)
Async XLA Ops:
  7.2 1.6 copy-start.9
  7.2 2.2 copy-start.11
  7.2 53.8 %all-gather.11.cloned.1.call-start = ((), (), s32[]{:S(2)}) async-start(), calls=%async_computation | async-start | bytes 9437184 | tf_op jit(solution)/shard_map/all_gather | solution.py:224
  7.9 103.3 %all-gather.15.cloned.1.call-start = ((), (), s32[]{:S(2)}) async-start(), calls=%async_computation.2 | async-start | bytes 9437184 | tf_op jit(solution)/shard_map/all_gather | solution.py:225
  8.7 154.6 %all-gather.17.cloned.1.call-start = ((), (), s32[]{:S(2)}) async-start(), calls=%async_computation.3 | async-start | bytes 1572864 | tf_op jit(solution)/shard_map/all_gather | solution.py:243
  23.0 3.8 %copy-start.2 = (bf16[2048,256]{1,0:T(8,128)(2,1)S(1)}, bf16[2048,256]{1,0:T(8,128)(2,1)}, u32[]{:S(2)}) copy-start(bf16[2048,256]{1,0:T(8,128)(2,1)} %param.15) | copy-start | bytes 3145732
  23.0 3.8 %copy-start.4 = (bf16[2048,256]{1,0:T(8,128)(2,1)S(1)}, bf16[2048,256]{1,0:T(8,128)(2,1)}, u32[]{:S(2)}) copy-start(bf16[2048,256]{1,0:T(8,128)(2,1)} %param.14) | copy-start | bytes 3145732
  27.1 1.5 copy-start.10
  154.3 1.5 copy-start.1
  157.0 44.8 %all-gather.21.cloned.1.call-start = ((), (), s32[]{:S(2)}) async-start(), calls=%async_computation.5 | async-start | bytes 2621440 | tf_op jit(solution)/shard_map/all_gather | solution.py:246
  169.8 2.5 copy-start
  171.1 80.7 %all-gather.19.cloned.1.call-start = ((), (), s32[]{:S(2)}) async-start(), calls=%async_computation.4 | async-start | bytes 9437184 | tf_op jit(solution)/shard_map/all_gather | solution.py:241
  171.7 140.9 %all-gather.13.cloned.1.call-start = ((), (), s32[]{:S(2)}) async-start(), calls=%async_computation.1 | async-start | bytes 9437184 | tf_op jit(solution)/shard_map/all_gather | solution.py:239
  210.4 7.4 %copy-start.6 = (bf16[4,2048,64]{1,2,0:T(8,128)(2,1)S(1)}, bf16[4,2048,64]{1,2,0:T(8,128)(2,1)}, u32[]{:S(2)}) copy-start(bf16[4,2048,64]{1,2,0:T(8,128)(2,1)} %copy.29) | copy-start | bytes 3145732
  263.3 6.2 %copy-start.5 = (bf16[2048,256]{1,0:T(8,128)(2,1)S(1)}, bf16[2048,256]{1,0:T(8,128)(2,1)}, u32[]{:S(2)}) copy-start(bf16[2048,256]{1,0:T(8,128)(2,1)} %param.14) | copy-start | bytes 3145732
  269.5 1.2 copy-start.3
  269.5 1.2 copy-start.8
  312.6 7.2 %copy-start.7 = (bf16[2048,2048]{1,0:T(8,128)(2,1)S(1)}, bf16[2048,2048]{1,0:T(8,128)(2,1)}, u32[]{:S(2)}) copy-start(bf16[2048,2048]{1,0:T(8,128)(2,1)} %all-gather.13.cloned.1.call-done) | copy-start | bytes 25165828
Sparse Core Ops, SparseCore 0:
  9.8 51.1 all-gather.10
  62.8 48.3 all-gather.14
  157.1 6.0 all-gather.16
  171.3 30.4 all-gather.20
  203.5 48.3 all-gather.18
  253.5 49.1 all-gather.12

commit v2 on v1

v2 whole, which is shorter than its diff:
```python
import functools
import math

import jax
import jax.numpy as jnp
from jax import lax
from jax.experimental import pallas as pl
from jax.experimental.pallas import tpu as pltpu
from jax.sharding import PartitionSpec as P

NORM_EPS = 1e-5
BLK = 256
HEADS = 4
DH = 64
NB = 8
CW = HEADS * BLK
EXP2_SCALE = (DH ** -0.5) * math.log2(math.e)
F32 = jnp.float32
BF16 = jnp.bfloat16


def seq_block(d):
    cp, half, sub = d // 4, (d // 2) % 2, d % 2
    return 2 * ((1 - half) * cp + half * (3 - cp)) + sub


def stored_block(j):
    b, sub = j // 2, j % 2
    half = b // 2
    cp = (1 - half) * b + half * (3 - b)
    return cp * 4 + half * 2 + sub


def nt_dot(a, b):
    return lax.dot_general(a, b, (((1,), (1,)), ((), ())), preferred_element_type=F32)


def dot(a, b):
    return jnp.dot(a, b, preferred_element_type=F32)


def rope_pairs(t, cos_t, sin_t):
    lane = lax.broadcasted_iota(jnp.int32, t.shape, 1)
    partner = jnp.where(lane % DH < DH // 2, pltpu.roll(t, 128 - DH // 2, 1), pltpu.roll(t, DH // 2, 1))
    return t * cos_t + partner * sin_t


def rows_of(b):
    return pl.ds(pl.multiple_of(b * BLK, BLK), BLK)


def causal_tile():
    row = lax.broadcasted_iota(jnp.int32, (BLK, CW), 0)
    col = lax.broadcasted_iota(jnp.int32, (BLK, CW), 1)
    return row <= col % BLK


MESH = pl.DeviceIdType.MESH
CHUNKS = 4


def neighbours():
    hp, cp = lax.axis_index('hp'), lax.axis_index('cp')
    flip = 1 - 2 * (hp % 2)
    y_hp = (hp + 2) % 4
    return hp, cp, hp + flip, y_hp, y_hp + flip


def tok_slot(hp, cp):
    return cp * 4 + hp


def head_slot(hp, cp):
    return hp * 2 + cp


def enter_barrier():
    hp, cp = lax.axis_index('hp'), lax.axis_index('cp')
    barrier = pltpu.get_barrier_semaphore()
    for m in range(1, 8):
        pl.semaphore_signal(barrier, inc=1, device_id=((hp + m // 2) % 4, (cp + m % 2) % 2), device_id_type=MESH)
    pl.semaphore_wait(barrier, 7)


class Gather:
    def __init__(self, src, dst, slot, send, recv, rows):
        self.src, self.dst, self.slot, self.send, self.recv = src, dst, slot, send, recv
        self.step = rows // CHUNKS
        self.hp, self.cp, self.xn, self.yn, self.dn = neighbours()

    def part(self, ref, c):
        return ref.at[pl.ds(c * self.step, self.step)]

    def place(self, hp, cp, c):
        return self.part(self.dst.at[self.slot(hp, cp)], c)

    def copy(self, kind, c):
        hp, cp, xn, yn, dn = self.hp, self.cp, self.xn, self.yn, self.dn
        origin, lands, to = {
            'own_x': (hp, 0, (xn, cp)), 'own_y': (hp, 1, (yn, cp)), 'own_s': (hp, 3, (hp, 1 - cp)),
            'x_s': (xn, 4, (hp, 1 - cp)), 'y_s': (yn, 5, (hp, 1 - cp)), 'd_s': (dn, 6, (hp, 1 - cp)),
            'x_y': (xn, 2, (yn, cp)), 'y_x': (yn, 2, (xn, cp)),
        }[kind]
        number = ('own_x', 'own_y', 'own_s', 'x_s', 'y_s', 'd_s', 'x_y', 'y_x').index(kind)
        src = self.part(self.src, c) if kind.startswith('own') else self.place(origin, cp, c)
        return pltpu.make_async_remote_copy(
            src_ref=src, dst_ref=self.place(origin, cp, c), send_sem=self.send.at[number, c],
            recv_sem=self.recv.at[lands, c], device_id=to, device_id_type=MESH)

    def await_from(self, number, c):
        hp, cp = ((self.xn, self.cp), (self.yn, self.cp), (self.dn, self.cp), (self.hp, 1 - self.cp),
                  (self.xn, 1 - self.cp), (self.yn, 1 - self.cp), (self.dn, 1 - self.cp))[number]
        ref = self.place(hp, cp, c)
        pltpu.make_async_remote_copy(
            src_ref=ref, dst_ref=ref, send_sem=self.send.at[0, c], recv_sem=self.recv.at[number, c],
            device_id=(self.hp, 1 - self.cp), device_id_type=MESH).wait_recv()

    def start_own(self):
        for c in range(CHUNKS):
            for kind in ('own_x', 'own_y', 'own_s'):
                self.copy(kind, c).start()

    def relay_near(self, chunks=range(CHUNKS)):
        for c in chunks:
            self.await_from(0, c)
            self.copy('x_s', c).start()
            if c < CHUNKS // 2:
                self.copy('x_y', c).start()
            self.await_from(1, c)
            self.copy('y_s', c).start()
            if c >= CHUNKS // 2:
                self.copy('y_x', c).start()

    def relay_diagonal(self):
        for c in range(CHUNKS):
            self.await_from(2, c)
            self.copy('d_s', c).start()

    def await_sibling(self, number):
        for c in range(CHUNKS):
            self.await_from(number, c)

    def finish_sends(self):
        for c in range(CHUNKS):
            for kind in ('own_x', 'own_y', 'own_s', 'x_s', 'y_s', 'd_s'):
                self.copy(kind, c).wait_send()
            self.copy('x_y' if c < CHUNKS // 2 else 'y_x', c).wait_send()


def gather_sems():
    return [pltpu.SemaphoreType.DMA((8, CHUNKS)), pltpu.SemaphoreType.DMA((7, CHUNKS))]


def unpack_table(tab):
    group = lax.broadcasted_iota(jnp.int32, tab.shape, 1) // (DH // 2)
    turned = [tab] + [pltpu.roll(tab, 32 * i, 1) for i in (1, 2, 3)]

    def pick(order):
        out = turned[order[3]]
        for g in range(3):
            out = jnp.where(group == g, turned[order[g]], out)
        return out

    sign = jnp.where(group % 2 == 0, -1.0, 1.0)
    cos_t = jnp.concatenate([pick((0, 1, 2, 3)), pick((2, 3, 0, 1))], axis=0)
    sin_t = jnp.concatenate([pick((3, 0, 1, 2)) * sign, pick((1, 2, 3, 0)) * sign], axis=0)
    return cos_t, sin_t


def project_block(d, x, gain, wq_ref, wkv_ref, tab, ht_ref, q_ref, k_ref, v_ref):
    xf = x.astype(F32)
    inv = lax.rsqrt(jnp.mean(xf * xf, axis=-1, keepdims=True) + NORM_EPS)
    h = (xf * inv * gain).astype(BF16)
    ht_ref[:, rows_of(d)] = h.T
    dst = rows_of(seq_block(d))
    cos_t, sin_t = unpack_table(tab)
    y = dot(h, wq_ref[...])
    for p in range(HEADS // 2):
        qr = rope_pairs(y[:, 128 * p:128 * (p + 1)], cos_t, sin_t).astype(BF16)
        q_ref[2 * p, dst, :] = qr[:, :DH]
        q_ref[2 * p + 1, dst, :] = qr[:, DH:]
    kv = dot(h, wkv_ref[...])
    k_ref[dst, :] = rope_pairs(kv, cos_t, sin_t).astype(BF16)[:, :DH]
    v_ref[dst, :] = kv.astype(BF16)[:, DH:]


def attend_block(j, q_ref, k_ref, vt_ref, e_ref, m_ref, ot_ref, lse_ref):
    q4 = q_ref[:, rows_of(j), :].reshape(CW, DH)

    def score_tile(kb, carry, masked):
        m_old, l_old = carry
        s = nt_dot(k_ref[rows_of(kb), :], q4) * EXP2_SCALE
        if masked:
            s = jnp.where(causal_tile(), s, -1e30)
        m_new = jnp.maximum(m_old, jnp.max(s, axis=0, keepdims=True))
        e = jnp.exp2(s - m_new)
        e_ref[rows_of(kb), :] = e
        m_ref[pl.ds(kb, 1), :] = m_new
        return m_new, l_old * jnp.exp2(m_old - m_new) + jnp.sum(e, axis=0, keepdims=True)

    carry = (jnp.full((1, CW), -1e30, F32), jnp.zeros((1, CW), F32))
    carry = score_tile(j, carry, True)
    m_fin, l_fin = lax.fori_loop(0, j, functools.partial(score_tile, masked=False), carry)
    inv_l = 1.0 / l_fin
    lse = m_fin + jnp.log2(l_fin)

    def out_tile(kb, acc):
        f = jnp.exp2(m_ref[pl.ds(kb, 1), :] - m_fin) * inv_l
        p = (e_ref[rows_of(kb), :] * f).astype(BF16)
        return acc + dot(vt_ref[:, rows_of(kb)], p)

    acc = lax.fori_loop(0, j + 1, out_tile, jnp.zeros((DH, CW), F32)).astype(BF16)
    dst = rows_of(stored_block(j))
    for h in range(HEADS):
        ot_ref[DH * h:DH * (h + 1), dst] = acc[:, BLK * h:BLK * (h + 1)]
        lse_ref[h:h + 1, rows_of(j)] = lse[:, BLK * h:BLK * (h + 1)]


def forward_kernel(x_own, dy_own, gain_ref, wq_hbm, wk_hbm, wv_hbm, tab_own,
                   dy_all, ht_out, q_ref, k_ref, v_ref, ot_ref, lse_ref, tabs,
                   xg, ht, e_ref, m_ref, vt_ref, wq, wk, wv, wkv, stage,
                   local_sem, tab_send, tab_recv, x_send, x_recv, dy_send, dy_recv):
    hp, cp, xn, yn, dn = neighbours()
    mine = tok_slot(hp, cp)
    hw = HEADS * DH
    loads = [
        pltpu.make_async_copy(x_own, xg.at[mine], local_sem.at[0]),
        pltpu.make_async_copy(wq_hbm.at[:, pl.ds(pl.multiple_of(head_slot(hp, cp) * hw, hw), hw)], wq, local_sem.at[1]),
        pltpu.make_async_copy(wk_hbm.at[:, pl.ds(pl.multiple_of((hp // 2) * 128, 128), 128)], wk, local_sem.at[2]),
        pltpu.make_async_copy(wv_hbm.at[:, pl.ds(pl.multiple_of((hp // 2) * 128, 128), 128)], wv, local_sem.at[3]),
        pltpu.make_async_copy(dy_own, stage, local_sem.at[4]),
        pltpu.make_async_copy(tab_own, tabs.at[mine], local_sem.at[5]),
    ]
    for load in loads:
        load.start()
    enter_barrier()
    gx = Gather(x_own, xg, tok_slot, x_send, x_recv, BLK)
    gdy = Gather(dy_own, dy_all, tok_slot, dy_send, dy_recv, BLK)

    def table_copy(m):
        to = ((hp + m // 2) % 4, (cp + m % 2) % 2)
        return pltpu.make_async_remote_copy(
            src_ref=tab_own, dst_ref=tabs.at[mine], send_sem=tab_send.at[m - 1], recv_sem=tab_recv.at[m - 1],
            device_id=to, device_id_type=MESH)

    for m in range(1, NB):
        table_copy(m).start()
    gx.start_own()
    for load in loads[1:4]:
        load.wait()
    lane = lax.broadcasted_iota(jnp.int32, wk.shape, 1)
    swap = hp % 2 == 1
    kf, vf = wk[...].astype(F32), wv[...].astype(F32)
    k_sel = jnp.where(swap, pltpu.roll(kf, DH, 1), kf)
    v_sel = jnp.where(swap, vf, pltpu.roll(vf, DH, 1))
    wkv[...] = jnp.where(lane < DH, k_sel, v_sel).astype(BF16)
    for i in (0, 4, 5):
        loads[i].wait()
    dy_mine = pltpu.make_async_copy(stage, dy_all.at[mine], local_sem.at[6])
    dy_mine.start()
    for m in range(1, NB):
        src_slot = tok_slot((hp + 4 - m // 2) % 4, (cp + m % 2) % 2)
        ref = tabs.at[src_slot]
        pltpu.make_async_remote_copy(
            src_ref=ref, dst_ref=ref, send_sem=tab_send.at[m - 1], recv_sem=tab_recv.at[m - 1],
            device_id=(hp, 1 - cp), device_id_type=MESH).wait_recv()

    def project(e, _):
        @pl.when(e == 1)
        def _():
            gx.await_sibling(3)

        @pl.when(e == 2)
        def _():
            gx.relay_near()
            gdy.start_own()

        @pl.when(e == 3)
        def _():
            gx.await_sibling(4)

        @pl.when(e == 5)
        def _():
            gx.await_sibling(5)

        @pl.when(e == 6)
        def _():
            gx.relay_diagonal()

        @pl.when(e == 7)
        def _():
            gx.await_sibling(6)

        m, b = e // 2, e % 2
        px = (hp % 2 + m % 2) % 2
        py = (hp // 2 + m // 2) % 2
        d = tok_slot(py * 2 + px, (cp + b) % 2)
        project_block(d, xg[d], gain_ref[...], wq, wkv, tabs[d], ht, q_ref, k_ref, v_ref)
        return 0

    lax.fori_loop(0, NB, project, 0)
    ht_copy = pltpu.make_async_copy(ht, ht_out, local_sem.at[7])
    ht_copy.start()
    vt_ref[...] = v_ref[...].T

    def attend(j, _):
        @pl.when(j == 5)
        def _():
            gdy.relay_near(range(0, CHUNKS // 2))

        @pl.when(j == 6)
        def _():
            gdy.relay_near(range(CHUNKS // 2, CHUNKS))

        attend_block(j, q_ref, k_ref, vt_ref, e_ref, m_ref, ot_ref, lse_ref)
        return 0

    lax.fori_loop(0, NB, attend, 0)
    gdy.relay_diagonal()
    for number in (3, 4, 5, 6):
        gdy.await_sibling(number)
    for m in range(1, NB):
        table_copy(m).wait_send()
    gx.finish_sends()
    gdy.finish_sends()
    dy_mine.wait()
    ht_copy.wait()


def backward_kernel(dy_all, wo_hbm, q_ref, k_ref, v_ref, ot_ref, lse_ref, tabs,
                    gq_ref, ot_all,
                    dyv, wo, do_ref, kt_ref, dk_ref, dv_ref, give, take,
                    local_sem, o_send, o_recv, pair_send, pair_recv):
    hp, cp, xn, yn, dn = neighbours()
    mine = head_slot(hp, cp)
    hw = HEADS * DH
    wo_load = pltpu.make_async_copy(wo_hbm.at[pl.ds(pl.multiple_of(mine * hw, hw), hw)], wo, local_sem.at[NB])
    wo_load.start()
    for d in range(NB):
        pltpu.make_async_copy(dy_all.at[d], dyv.at[d], local_sem.at[d]).start()
    ot_mine = pltpu.make_async_copy(ot_ref, ot_all.at[mine], local_sem.at[NB + 1])
    ot_mine.start()
    enter_barrier()
    go = Gather(ot_ref, ot_all, head_slot, o_send, o_recv, hw)
    go.start_own()
    kt_ref[...] = k_ref[...].T
    dk_ref[...] = jnp.zeros_like(dk_ref)
    dv_ref[...] = jnp.zeros_like(dv_ref)
    wo_load.wait()

    def project(d, _):
        pltpu.make_async_copy(dy_all.at[d], dyv.at[d], local_sem.at[d]).wait()
        do = nt_dot(dyv[d], wo[...]).astype(BF16)
        dst = rows_of(seq_block(d))
        for h in range(HEADS):
            do_ref[h, dst, :] = do[:, DH * h:DH * (h + 1)]
        return 0

    lax.fori_loop(0, NB, project, 0)

    def attend(j, _):
        @pl.when(j == 5)
        def _():
            go.relay_near(range(0, CHUNKS // 2))

        @pl.when(j == 6)
        def _():
            go.relay_near(range(CHUNKS // 2, CHUNKS))

        slot = stored_block(j)
        src = rows_of(slot)
        q4 = q_ref[:, rows_of(j), :].reshape(CW, DH)
        do4 = do_ref[:, rows_of(j), :].reshape(CW, DH)
        o4t = jnp.concatenate([ot_ref[DH * h:DH * (h + 1), src] for h in range(HEADS)], axis=1)
        lse = jnp.concatenate([lse_ref[h:h + 1, rows_of(j)] for h in range(HEADS)], axis=1)
        delta = jnp.sum(do4.astype(F32).T * o4t.astype(F32), axis=0, keepdims=True)

        def tile(kb, dqt, masked):
            keys = rows_of(kb)
            p = jnp.exp2(nt_dot(k_ref[keys, :], q4) * EXP2_SCALE - lse)
            if masked:
                p = jnp.where(causal_tile(), p, 0.0)
            dp = nt_dot(v_ref[keys, :], do4)
            dv_ref[keys, :] += dot(p.astype(BF16), do4)
            ds = (p * (dp - delta)).astype(BF16)
            dk_ref[keys, :] += dot(ds, q4)
            return dqt + dot(kt_ref[:, keys], ds)

        dqt = tile(j, jnp.zeros((DH, CW), F32), True)
        dqt = lax.fori_loop(0, j, functools.partial(tile, masked=False), dqt) * (DH ** -0.5)
        cos_t, sin_t = unpack_table(tabs[slot])
        for p in range(HEADS // 2):
            pair = jnp.concatenate([dqt[:, BLK * (2 * p):BLK * (2 * p + 1)], dqt[:, BLK * (2 * p + 1):BLK * (2 * p + 2)]], axis=0)
            dq = pair.T.astype(BF16).astype(F32)
            gq_ref[src, 128 * p:128 * (p + 1)] = rope_pairs(dq, cos_t, -sin_t).astype(BF16)
        return 0

    lax.fori_loop(0, NB, attend, 0)
    give[:, :DH] = (dk_ref[...] * (DH ** -0.5)).astype(BF16)
    give[:, DH:] = dv_ref[...].astype(BF16)
    swap = pltpu.make_async_remote_copy(
        src_ref=give, dst_ref=take, send_sem=pair_send, recv_sem=pair_recv, device_id=(hp, 1 - cp), device_id_type=MESH)
    swap.start()
    go.relay_diagonal()
    swap.wait_recv()
    lane = lax.broadcasted_iota(jnp.int32, (BLK, 2 * DH), 1)
    for i in range(NB // 2):
        slot = cp * 4 + i
        src = rows_of(seq_block(slot))
        total = (give[src, :].astype(F32) + take[src, :].astype(F32)).astype(BF16).astype(F32)
        cos_t, sin_t = unpack_table(tabs[slot])
        turned = rope_pairs(total, cos_t, -sin_t)
        gq_ref[pl.ds(NB * BLK + (i % 2) * BLK, BLK), 128 * (i // 2):128 * (i // 2 + 1)] = jnp.where(lane < DH, turned, total).astype(BF16)
    for number in (3, 4, 5, 6):
        go.await_sibling(number)
    swap.wait_send()
    go.finish_sends()
    ot_mine.wait()


VMEM_SPEC = pl.BlockSpec(memory_space=pltpu.VMEM)
ANY_SPEC = pl.BlockSpec(memory_space=pl.ANY)


def run_forward(x_own, dy_own, gain, w_q, w_k, w_v, tab):
    rows, width = x_own.shape
    toks = rows * NB
    hw = HEADS * DH
    return pl.pallas_call(
        forward_kernel,
        out_shape=(
            jax.ShapeDtypeStruct((NB, rows, width), BF16),
            jax.ShapeDtypeStruct((width, toks), BF16),
            jax.ShapeDtypeStruct((HEADS, toks, DH), BF16),
            jax.ShapeDtypeStruct((toks, DH), BF16),
            jax.ShapeDtypeStruct((toks, DH), BF16),
            jax.ShapeDtypeStruct((hw, toks), BF16),
            jax.ShapeDtypeStruct((HEADS, toks), F32),
            jax.ShapeDtypeStruct((NB, 128, 128), F32),
        ),
        in_specs=[ANY_SPEC, ANY_SPEC, VMEM_SPEC, ANY_SPEC, ANY_SPEC, ANY_SPEC, ANY_SPEC],
        out_specs=(ANY_SPEC, ANY_SPEC) + (VMEM_SPEC,) * 6,
        scratch_shapes=[
            pltpu.VMEM((NB, rows, width), BF16), pltpu.VMEM((width, toks), BF16),
            pltpu.VMEM((toks, CW), F32), pltpu.VMEM((NB, CW), F32), pltpu.VMEM((DH, toks), BF16),
            pltpu.VMEM((width, hw), BF16), pltpu.VMEM((width, 128), BF16), pltpu.VMEM((width, 128), BF16),
            pltpu.VMEM((width, 128), BF16), pltpu.VMEM((rows, width), BF16),
            pltpu.SemaphoreType.DMA((8,)), pltpu.SemaphoreType.DMA((7,)), pltpu.SemaphoreType.DMA((7,)),
        ] + gather_sems() + gather_sems(),
        compiler_params=pltpu.CompilerParams(vmem_limit_bytes=60 * 1024 * 1024, collective_id=0, has_side_effects=True),
        cost_estimate=pl.CostEstimate(flops=30_000_000_000, bytes_accessed=20_000_000, transcendentals=0),
        name="attn_forward",
    )(x_own, dy_own, gain, w_q, w_k, w_v, tab)


def run_backward(dy_all, w_o, q, k, v, o_t, lse, tabs):
    _, rows, width = dy_all.shape
    toks = rows * NB
    hw = HEADS * DH
    return pl.pallas_call(
        backward_kernel,
        out_shape=(
            jax.ShapeDtypeStruct((toks + 2 * BLK, hw), BF16),
            jax.ShapeDtypeStruct((NB, hw, toks), BF16),
        ),
        in_specs=[ANY_SPEC, ANY_SPEC] + [VMEM_SPEC] * 6,
        out_specs=(VMEM_SPEC, ANY_SPEC),
        scratch_shapes=[
            pltpu.VMEM((NB, rows, width), BF16), pltpu.VMEM((hw, width), BF16),
            pltpu.VMEM((HEADS, toks, DH), BF16), pltpu.VMEM((DH, toks), BF16),
            pltpu.VMEM((toks, DH), F32), pltpu.VMEM((toks, DH), F32),
            pltpu.VMEM((toks, 2 * DH), BF16), pltpu.VMEM((toks, 2 * DH), BF16),
            pltpu.SemaphoreType.DMA((NB + 2,)),
        ] + gather_sems() + [pltpu.SemaphoreType.DMA, pltpu.SemaphoreType.DMA],
        compiler_params=pltpu.CompilerParams(vmem_limit_bytes=60 * 1024 * 1024, collective_id=1, has_side_effects=True),
        cost_estimate=pl.CostEstimate(flops=40_000_000_000, bytes_accessed=20_000_000, transcendentals=0),
        name="attn_backward",
    )(dy_all, w_o, q, k, v, o_t, lse, tabs)


def solution(mesh):
    def device_step(hidden, grad_out, positions, norm_gain, w_q, w_k, w_v, w_o, inv_freq):
        rows = hidden.shape[0]
        toks = rows * NB
        hw = HEADS * DH
        hp, cp = lax.axis_index('hp'), lax.axis_index('cp')
        me_tok = tok_slot(hp, cp)
        angles = positions.astype(F32)[:, None] * inv_freq[None, :]
        cos_h, sin_h = jnp.cos(angles), jnp.sin(angles)
        tab = jnp.concatenate([cos_h[:128], sin_h[:128], cos_h[128:], sin_h[128:]], axis=1)
        gain = norm_gain.astype(F32)[None, :]
        dy_all, h_t, q, k, v, o_t, lse, tabs = run_forward(hidden, grad_out, gain, w_q, w_k, w_v, tab)
        gq_ext, ot_all = run_backward(dy_all, w_o, q, k, v, o_t, lse, tabs)
        ot_all = ot_all.reshape(NB * hw, toks)
        ext = lax.all_gather(gq_ext, ('hp', 'cp'), axis=0)
        gq_cols = ext[:, :toks].transpose(1, 0, 2).reshape(toks, NB * hw)
        gkv = ext[:, toks:].reshape(4, 2, 2 * BLK, 2, 2 * DH).transpose(0, 1, 3, 2, 4).reshape(4, toks, 2 * DH)
        gk_cols = gkv[:, :, :DH].transpose(1, 0, 2).reshape(toks, 4 * DH)
        gv_cols = gkv[:, :, DH:].transpose(1, 0, 2).reshape(toks, 4 * DH)
        x_f32 = hidden.astype(F32)
        inv_rms = lax.rsqrt(jnp.mean(x_f32 * x_f32, axis=-1, keepdims=True) + NORM_EPS)
        x_hat = x_f32 * inv_rms
        o_mine = lax.dynamic_slice_in_dim(ot_all, me_tok * rows, rows, 1)
        output = (x_f32 + jnp.einsum('at,ab->tb', o_mine, w_o, preferred_element_type=F32)).astype(BF16)
        grad_wo = jnp.dot(ot_all, dy_all.reshape(toks, -1), preferred_element_type=F32)
        grad_wq = jnp.dot(h_t, gq_cols, preferred_element_type=F32)
        grad_wk = jnp.dot(h_t, gk_cols, preferred_element_type=F32)
        grad_wv = jnp.dot(h_t, gv_cols, preferred_element_type=F32)
        mine = lambda a: lax.dynamic_slice_in_dim(a, me_tok * rows, rows, 0)
        d_norm = (jnp.einsum('tb,ab->ta', mine(gq_cols), w_q, preferred_element_type=F32)
                  + jnp.einsum('tb,ab->ta', mine(gk_cols), w_k, preferred_element_type=F32)
                  + jnp.einsum('tb,ab->ta', mine(gv_cols), w_v, preferred_element_type=F32))
        gain_part = jnp.sum(d_norm * x_hat, axis=0, keepdims=True)
        grad_gain = jnp.sum(lax.all_gather(gain_part, ('cp', 'hp'), axis=0, tiled=True), axis=0)
        d_hat = d_norm * gain
        grad_hidden = (grad_out.astype(F32) + inv_rms * (d_hat - x_hat * jnp.mean(d_hat * x_hat, axis=-1, keepdims=True))).astype(BF16)
        return output, grad_hidden, grad_wq, grad_wk, grad_wv, grad_wo, grad_gain

    seq_spec = P(('cp', 'hp'), None)
    whole = P()
    return jax.shard_map(device_step, mesh=mesh, in_specs=(seq_spec, seq_spec, P(('cp', 'hp')), whole, whole, whole, whole, whole, whole), out_specs=(seq_spec, seq_spec, whole, whole, whole, whole, whole), check_vma=False)
```

time: 349 us -> 305 us (0.87)
  waiting for transfers between devices: 94.2 us -> 27.3 us
  Pallas kernels: 89.4 us -> 133 us
  other arithmetic: 22.9 us -> 7.7 us
  blocking collectives: 25.7 us -> 11 us
  local copies, waits for them, and re-layouts: 25.1 us -> 35.4 us
    all_gather x6 -> x1, waiting for transfers between devices: 91.8 us -> 27.3 us  [device_step(): ext = lax.all_gather(gq_ext, ('hp', 'cp'), axis=0)]
    pallas_call x2, Pallas kernels: 89.4 us -> 133 us  [the longest x1 85.7 us: run_forward(): pl.pallas_call(forward_kernel, out_shape=(jax.ShapeDtypeStruct((NB, rows,...]
    all_gather x1 -> x0, blocking collectives: 13.6 us -> none  [device_step(): pos_all = lax.all_gather(positions, ('cp', 'hp'), axis=0, tiled=True)]
    all_gather x1 -> x0, local copies, waits for them, and re-layouts: 11.4 us -> none  [device_step(): gq_all = lax.all_gather(g_q, ('hp', 'cp'), axis=0)]
    unnamed x26 -> x24, local copies, waits for them, and re-layouts: 5.21 us -> 16.1 us
    transpose x0 -> x4, local copies, waits for them, and re-layouts: none -> 10.2 us  [the longest x2 5.63 us: device_step(): gv_cols = gkv[:, :, DH:].transpose(1, 0, 2).reshape(toks, 4 * DH)]
    concatenate x6 -> x1, other arithmetic: 6.87 us -> 0.75 us  [device_step(): jnp.concatenate([cos_h[:128], sin_h[:128], cos_h[128:], sin_h[128:]], axi...]
    another operation x1 -> x0, other arithmetic: 4.81 us -> none
  transfers between devices with their start and end apart: 6 -> 1, of which waited for: 5 -> 1; matrix products, arithmetic and copies ran while one was open for 24% -> 9% of each run, Pallas kernels for 13% -> 0%
where the time goes in v2:
time: 305 us; the launch traced here: 304 us
  Pallas kernels  133 us (44%)
  matrix products  75.7 us (25%)
  local copies, waits for them, and re-layouts  35.4 us (12%)
  waiting for transfers between devices  27.3 us (9%)
  between operations  14.2 us (5%)
  blocking collectives  11 us (4%)
  other arithmetic  7.7 us (3%)
    pallas_call x1, Pallas kernels, run_forward(): pl.pallas_call(forward_kernel, out_shape=(jax.ShapeDtypeStruct((NB, rows,...  85.7 us
    pallas_call x1, Pallas kernels, run_backward(): pl.pallas_call(backward_kernel, out_shape=(jax.ShapeDtypeStruct((toks + 2...  47.2 us
    all_gather x1, waiting for transfers between devices, device_step(): ext = lax.all_gather(gq_ext, ('hp', 'cp'), axis=0)  27.3 us
    dot_general x1, matrix products, device_step(): grad_wq = jnp.dot(h_t, gq_cols, preferred_element_type=F32)  24.4 us
    dot_general x1, matrix products, device_step(): jnp.dot(ot_all, dy_all.reshape(toks, -1), preferred_element_type=F32)  20.6 us
    unnamed x24, local copies, waits for them, and re-layouts  16.1 us
    all_gather x1, blocking collectives, device_step(): lax.all_gather(gain_part, ('cp', 'hp'), axis=0, tiled=True)  11 us
    dot_general x1, matrix products, device_step(): jnp.einsum('tb,ab->ta', mine(gq_cols), w_q, preferred_element_type=F32)  7.45 us
  transfers between devices with their start and end apart: 1, of which 1 were waited for; matrix products, arithmetic and copies ran while one was open for 9% of the time, Pallas kernels for 0%

profile of v2, /device:TPU:0, one launch (start us, length us, event | category | flops | bytes accessed | tf_op | source)
XLA Modules:
  0.0 304.3 jit_solution(3436012138343669833)
XLA Ops:
  7.2 0.0 all-gather.4.cloned.1.call-start
  7.2 0.7 convert_element_type.20
  7.9 1.3 convert_element_type.19
  9.2 1.2 multiply_cosine_fusion
  10.4 0.8 pad_maximum_fusion.tab_own
  11.2 85.7 %attn_forward.1 = (bf16[8,256,2048]{2,1,0:T(8,128)(2,1)}, bf16[2048,2048]{1,0:T(8,128)(2,1)}, bf16[4,2048,64]{2,1,0:T(8,128)(2,1)}, bf16[2048,64]{1,0:T(8,128)(2...) custom-call(bf16[256,2048]{1,0:T(8,128)(2,1)} %x_own.1, ...), custom_call_target="tpu_custom_call" | custom-call | flops 30000001024 | bytes 20000000 | tf_op jit(solution)/shard_map/attn_forward/pallas_call | solution.py:429
  96.9 0.0 copy-start
  96.9 47.2 %attn_backward.1 = (bf16[2560,256]{1,0:T(8,128)(2,1)}, bf16[8,256,2048]{2,1,0:T(8,128)(2,1)}) custom-call(bf16[8,256,2048]{2,1,0:T(8,128)(2,1)} %get-tuple-element.17.dy_all, bf16[2048,2048]{1,0:T(8,128)(2,1)} %wo_hbm.1, bf16[4,2048,64]{2,1,0:T(8,128)(2,1)} %get-tuple-element.18.q_ref, bf16[2048,64]{1,0:T(8,128)(2,1)} %get-tuple-element.19.k_ref, ...), custom_call_target="tpu_custom_call" | custom-call | flops 40000000000 | bytes 20000000 | tf_op jit(solution)/shard_map/attn_backward/pallas_call | solution.py:460
  144.1 0.0 all-gather.4.cloned.1.call-update
  144.2 0.0 copy-done
  144.2 0.0 slice-start
  144.2 0.3 fusion.10
  144.5 0.0 slice-start.1
  144.5 0.0 copy-start.8
  144.5 7.2 %fusion.3 = bf16[256,2048]{1,0:T(8,128)(2,1)} fusion(bf16[2048,2048]{1,0:T(8,128)(2,1)} %wo_hbm.1, bf16[256,2048]{1,0:T(8,128)(2,1)S(1)} %copy-done, bf16[2048,2048]{1,0:T(8,128)(2,1)} %bitcast.39, s32[]{:T(128)S(6)} %select_n.2), kind=kOutput, calls=%fused_computation.8 | convolution fusion | flops 2149056512 | bytes 11534340 | tf_op jit(solution)/shard_map/at,ab->tb/dot_general | solution.py:504
  151.7 0.0 slice-done
  151.7 0.0 slice-done.1
  151.7 1.5 copy-done.8
  153.2 20.6 %fusion.25 = f32[2048,2048]{1,0:T(8,128)} fusion(bf16[2048,2048]{1,0:T(8,128)(2,1)S(1)} %bitcast.42, bf16[2048,2048]{1,0:T(8,128)(2,1)S(1)} %bitcast.44), kind=kOutput, calls=%fused_computation.37 | convolution fusion | flops 17179869184 | bytes 33554432 | tf_op jit(solution)/shard_map/dot_general | solution.py:505
  173.8 27.3 %all-gather.4.cloned.1.call-done = bf16[20480,256]{1,0:T(8,128)(2,1)} async-done(((bf16[2560,256]{1,0:T(8,128)(2,1)}), bf16[20480,256]{1,0:T(8,128)(2,1)}) %all-gather.4.cloned.1.call-update) | async-done | bytes 10485776 | tf_op jit(solution)/shard_map/all_gather | solution.py:495
  201.1 1.7 slice.37
  202.9 7.3 %slice.36 = bf16[8,2048,256]{2,1,0:T(8,128)(2,1)} slice(bf16[8,2560,256]{2,1,0:T(8,128)(2,1)} %bitcast.31), slice={[0:8], [0:2048], [0:256]} | slice | bytes 16777216 | tf_op jit(solution)/shard_map/slice | solution.py:496
  210.2 11.4 %copy.34 = bf16[8,2048,256]{1,2,0:T(8,128)(2,1)} copy(bf16[8,2048,256]{2,1,0:T(8,128)(2,1)} %slice.36) | data formatting | bytes 16777216
  221.6 2.4 copy.35
  224.0 3.0 copy.31
  227.0 7.5 %fusion.11 = f32[256,2048]{1,0:T(8,128)} fusion(bf16[2048,2048]{1,0:T(8,128)(2,1)} %wq_hbm.1, bf16[2048,2048]{0,1:T(8,128)(2,1)} %bitcast.32, s32[]{:T(128)S(6)} %select_n.2), kind=kOutput, calls=%fused_computation.18 | convolution fusion | flops 2147483648 | bytes 11534340 | tf_op jit(solution)/shard_map/tb,ab->ta/dot_general | solution.py:510
  234.4 2.7 slice_bitcast_fusion
  237.2 0.0 copy-start.1
  237.2 2.9 copy.33
  240.1 0.0 copy-done.1
  240.1 1.6 copy.32
  241.7 0.0 copy-start.4
  241.7 24.4 %fusion.22 = f32[2048,2048]{1,0:T(8,128)} fusion(bf16[2048,2048]{1,0:T(8,128)(2,1)} %get-tuple-element.26, bf16[2048,2048]{0,1:T(8,128)(2,1)} %bitcast.33), kind=kOutput, calls=%fused_computation.34 | convolution fusion | flops 17179869184 | bytes 33554432 | tf_op jit(solution)/shard_map/dot_general | solution.py:506
  266.1 0.0 copy-done.4
  266.1 0.0 copy-start.2
  266.1 0.0 copy-start.6
  266.1 7.2 %fusion.23 = f32[2048,256]{1,0:T(8,128)} fusion(bf16[2048,2048]{1,0:T(8,128)(2,1)} %get-tuple-element.26, bf16[2048,256]{0,1:T(8,128)(2,1)S(1)} %bitcast.37), kind=kOutput, calls=%fused_computation.35 | convolution fusion | flops 2147483648 | bytes 11534336 | tf_op jit(solution)/shard_map/dot_general | solution.py:507
  273.4 0.0 copy-done.2
  273.4 0.0 copy-done.6
  273.4 0.5 convolution_add_fusion.1
  273.9 0.7 copy-done.3
  274.6 7.2 %fusion.24 = f32[2048,256]{1,0:T(8,128)} fusion(bf16[2048,2048]{1,0:T(8,128)(2,1)} %get-tuple-element.26, bf16[2048,256]{0,1:T(8,128)(2,1)S(1)} %bitcast.35), kind=kOutput, calls=%fused_computation.36 | convolution fusion | flops 2147483648 | bytes 11534336 | tf_op jit(solution)/shard_map/dot_general | solution.py:508
  281.8 0.0 copy-done.5
  281.8 0.0 copy-done.7
  281.8 1.1 fusion.9
  282.8 11.0 %all-gather.1 = f32[16384]{0:T(1024)S(1)} all-gather(f32[2048]{0:T(1024)S(1)} %get-tuple-element.27), channel_id=3, replica_groups=mesh['hp'=4,'cp'=2] {'cp','hp'}, dimensions={0}, use_global_device_ids=true | all-gather | bytes 73728 | tf_op jit(solution)/shard_map/all_gather | solution.py:514
  293.9 2.9 fusion.8
  296.8 0.6 reduce_sum.39
  (8 shorter events, 0.1 us)
Async XLA Ops:
  7.2 194.0 %all-gather.4.cloned.1.call-start = ((), (), s32[]{:S(2)}) async-start(), calls=%async_computation | async-start | bytes 11796480 | tf_op jit(solution)/shard_map/all_gather | solution.py:495
  96.9 47.3 %copy-start = (bf16[256,2048]{1,0:T(8,128)(2,1)S(1)}, bf16[256,2048]{1,0:T(8,128)(2,1)}, u32[]{:S(2)}) copy-start(bf16[256,2048]{1,0:T(8,128)(2,1)} %x_own.1) | copy-start | bytes 3145732
  144.2 7.5 %slice-start = ((s8[8388608]{0:T(1024)(128)(4,1)}), s8[4194304]{0:T(1024)(128)(4,1)S(1)}, s32[]{:S(2)}) async-start(s8[8388608]{0:T(1024)(128)(4,1)} %bitcast.40), calls=%async_computation.1 | async-start | bytes 8388608
  144.5 7.2 %slice-start.1 = ((s8[8388608]{0:T(1024)(128)(4,1)}), s8[4194304]{0:T(1024)(128)(4,1)S(1)}, s32[]{:S(2)}) async-start(s8[8388608]{0:T(1024)(128)(4,1)} %bitcast.40), calls=%async_computation.2 | async-start | bytes 8388608
  144.5 8.7 %copy-start.8 = (bf16[8,256,2048]{2,1,0:T(8,128)(2,1)S(1)}, bf16[8,256,2048]{2,1,0:T(8,128)(2,1)}, u32[]{:S(2)}) copy-start(bf16[8,256,2048]{2,1,0:T(8,128)(2,1)} %get-tuple-element.17.dy_all) | copy-start | bytes 25165828
  237.2 2.9 copy-start.1
  241.7 24.4 %copy-start.4 = (bf16[2048,4,64]{0,2,1:T(8,128)(2,1)S(1)}, bf16[2048,4,64]{0,2,1:T(8,128)(2,1)}, u32[]{:S(2)}) copy-start(bf16[2048,4,64]{0,2,1:T(8,128)(2,1)} %copy.32) | copy-start | bytes 3145732
  266.1 7.3 %copy-start.2 = (f32[256,2048]{1,0:T(8,128)S(1)}, f32[256,2048]{1,0:T(8,128)}, u32[]{:S(2)}) copy-start(f32[256,2048]{1,0:T(8,128)} %fusion.11) | copy-start | bytes 6291460
  266.1 7.3 %copy-start.6 = (bf16[2048,256]{1,0:T(8,128)(2,1)S(1)}, bf16[2048,256]{1,0:T(8,128)(2,1)}, u32[]{:S(2)}) copy-start(bf16[2048,256]{1,0:T(8,128)(2,1)} %wk_hbm.1) | copy-start | bytes 3145732
  273.4 1.2 copy-start.3
  274.6 7.2 %copy-start.5 = (bf16[2048,256]{1,0:T(8,128)(2,1)S(1)}, bf16[2048,256]{1,0:T(8,128)(2,1)}, u32[]{:S(2)}) copy-start(bf16[2048,256]{1,0:T(8,128)(2,1)} %wv_hbm.1) | copy-start | bytes 3145732
  274.6 7.2 %copy-start.7 = (f32[2048]{0:T(1024)S(1)}, f32[2048]{0:T(1024)}, u32[]{:S(2)}) copy-start(f32[2048]{0:T(1024)} %convert_element_type.19) | copy-start | bytes 24580
Sparse Core Ops, SparseCore 0:
  144.3 56.8 all-gather.3

commit v3 on v2

--- a/solution.py
+++ b/solution.py
@@ -328,7 +328,7 @@
 
 
 def backward_kernel(dy_all, wo_hbm, q_ref, k_ref, v_ref, ot_ref, lse_ref, tabs,
-                    gq_ref, ot_all,
+                    gq_ref, gkv_ref, ot_all,
                     dyv, wo, do_ref, kt_ref, dk_ref, dv_ref, give, take,
                     local_sem, o_send, o_recv, pair_send, pair_recv):
     hp, cp, xn, yn, dn = neighbours()
@@ -410,12 +410,186 @@
         total = (give[src, :].astype(F32) + take[src, :].astype(F32)).astype(BF16).astype(F32)
         cos_t, sin_t = unpack_table(tabs[slot])
         turned = rope_pairs(total, cos_t, -sin_t)
-        gq_ref[pl.ds(NB * BLK + (i % 2) * BLK, BLK), 128 * (i // 2):128 * (i // 2 + 1)] = jnp.where(lane < DH, turned, total).astype(BF16)
+        gkv_ref[(i % 2) * BLK:(i % 2 + 1) * BLK, 128 * (i // 2):128 * (i // 2 + 1)] = jnp.where(lane < DH, turned, total).astype(BF16)
     for number in (3, 4, 5, 6):
         go.await_sibling(number)
     swap.wait_send()
     go.finish_sends()
     ot_mine.wait()
+
+
+def nth_peer(e):
+    hp, cp = lax.axis_index('hp'), lax.axis_index('cp')
+    m, b = e // 2, e % 2
+    px = (hp % 2 + m % 2) % 2
+    py = (hp // 2 + m // 2) % 2
+    return py * 2 + px, (cp + b) % 2
+
+
+def weight_grad(a_ref, b, stage):
+    def rows(i, _):
+        a = a_ref[pl.ds(2 * i, 2)].reshape(2 * BLK, NB * BLK)
+        stage[pl.ds(pl.multiple_of(i * 2 * BLK, 2 * BLK), 2 * BLK), :] = dot(a, b)
+        return 0
+
+    lax.fori_loop(0, NB // 2, rows, 0)
+
+
+def grads_kernel(gq_own, gkv_own, ot_hbm, dy_hbm, ht_hbm, wo_hbm, wq_hbm, wk_hbm, wv_hbm, x_ref, dy_ref, gain_ref,
+                 out_ref, gh_ref, gq_all, gwo_hbm, gwk_ref, gwv_ref, gg_ref,
+                 gkvg, ot, dya, wbuf, wk, wv, stage, acc, o_mine, gq_mine, bk, bv, pass_gq, gains,
+                 local_sem, stage_sem, mine_sem, q_send, q_recv, kv_send, kv_recv, gain_send, gain_recv):
+    hp, cp, xn, yn, dn = neighbours()
+    me_tok, me_head = tok_slot(hp, cp), head_slot(hp, cp)
+    my_rows = rows_of(me_tok)
+    copy = pltpu.make_async_copy
+    loads = dict(
+        ot=copy(ot_hbm, ot, local_sem.at[0]), wo=copy(wo_hbm, wbuf, local_sem.at[1]),
+        dy=copy(dy_hbm, dya, local_sem.at[2]), gq=copy(gq_own, pass_gq, local_sem.at[3]),
+        gkv=copy(gkv_own, gkvg.at[me_head], local_sem.at[4]),
+        wk=copy(wk_hbm, wk, local_sem.at[5]), wv=copy(wv_hbm, wv, local_sem.at[6]))
+    for name in ('gkv', 'ot', 'wo', 'gq', 'dy', 'wk', 'wv'):
+        loads[name].start()
+    enter_barrier()
+    gkv = Gather(gkv_own, gkvg, head_slot, kv_send, kv_recv, 2 * BLK)
+    ggq = Gather(gq_own, gq_all, head_slot, q_send, q_recv, NB * BLK)
+    gkv.start_own()
+    ggq.start_own()
+    loads['gq'].wait()
+    keep_gq = copy(pass_gq, gq_all.at[me_head], local_sem.at[7])
+    keep_gq.start()
+
+    loads['ot'].wait()
+
+    def turn(d, _):
+        o_mine[:, rows_of(d)] = ot[d, :, my_rows].T
+        return 0
+
+    lax.fori_loop(0, NB, turn, 0)
+    loads['wo'].wait()
+
+    def out_cols(n, _):
+        cols = rows_of(n)
+        out_ref[:, cols] = (x_ref[:, cols].astype(F32) + dot(o_mine[...], wbuf[:, cols])).astype(BF16)
+        return 0
+
+    lax.fori_loop(0, NB, out_cols, 0)
+    wq_load = copy(wq_hbm, wbuf, local_sem.at[8])
+    wq_load.start()
+    gkv.relay_near()
+    loads['dy'].wait()
+
+    def stage_out(n, slot):
+        return copy(stage.at[slot], gwo_hbm.at[:, rows_of(n)], stage_sem.at[slot])
+
+    def wo_cols(n, _):
+        @pl.when(n == 1)
+        def _():
+            gkv.relay_diagonal()
+
+        @pl.when(n == 3)
+        def _():
+            ggq.relay_near(range(0, CHUNKS // 2))
+
+        slot = n % 2
+
+        @pl.when(n >= 2)
+        def _():
+            stage_out(n - 2, slot).wait()
+
+        weight_grad(ot, dya[:, :, rows_of(n)].reshape(NB * BLK, BLK), stage.at[slot])
+        stage_out(n, slot).start()
+        return 0
+
+    lax.fori_loop(0, NB, wo_cols, 0)
+    ht_load = copy(ht_hbm, dya, local_sem.at[9])
+    ht_load.start()
+    ggq.relay_near(range(CHUNKS // 2, CHUNKS))
+
+    for number in (3, 4, 5, 6):
+        gkv.await_sibling(number)
+    loads['gkv'].wait()
+    for c in range(2):
+        for r in range(2):
+            dst = pl.ds((c * 2 + r) * 2 * BLK, 2 * BLK)
+            for p in range(2):
+                even = gkvg[4 * p + c, :, 128 * r:128 * (r + 1)]
+                odd = gkvg[4 * p + 2 + c, :, 128 * r:128 * (r + 1)]
+                bk[dst, 128 * p:128 * (p + 1)] = jnp.concatenate([even[:, :DH], odd[:, :DH]], axis=1)
+                bv[dst, 128 * p:128 * (p + 1)] = jnp.concatenate([even[:, DH:], odd[:, DH:]], axis=1)
+    ht_load.wait()
+    weight_grad(dya, bk[...], gwk_ref)
+    weight_grad(dya, bv[...], gwv_ref)
+
+    loads['wk'].wait()
+    loads['wv'].wait()
+    acc[...] = nt_dot(bk[my_rows, :], wk[...]) + nt_dot(bv[my_rows, :], wv[...])
+    wq_load.wait()
+    keep_gq.wait()
+    for number in (3, 4, 5):
+        ggq.await_sibling(number)
+
+    def fetch(e):
+        return copy(gq_all.at[head_slot(*nth_peer(e)), my_rows], gq_mine.at[e], mine_sem.at[e])
+
+    def add_head(e, _):
+        fetch(e).wait()
+        cols = rows_of(head_slot(*nth_peer(e)))
+        acc[...] += nt_dot(gq_mine[e], wbuf[:, cols])
+        return 0
+
+    for e in range(6):
+        fetch(e).start()
+    lax.fori_loop(0, 6, add_head, 0)
+    ggq.relay_diagonal()
+    fetch(6).start()
+    ggq.await_sibling(6)
+    fetch(7).start()
+    lax.fori_loop(6, NB, add_head, 0)
+
+    x = x_ref[...].astype(F32)
+    inv = lax.rsqrt(jnp.mean(x * x, axis=-1, keepdims=True) + NORM_EPS)
+    x_hat = x * inv
+    d_norm = acc[...]
+    gains[me_tok] = jnp.sum(d_norm * x_hat, axis=0, keepdims=True)
+
+    def gain_copy(m):
+        return pltpu.make_async_remote_copy(
+            src_ref=gains.at[me_tok], dst_ref=gains.at[me_tok], send_sem=gain_send.at[m - 1], recv_sem=gain_recv.at[m - 1],
+            device_id=((hp + m // 2) % 4, (cp + m % 2) % 2), device_id_type=MESH)
+
+    d_hat = d_norm * gain_ref[...]
+    row_mean = jnp.mean(d_hat * x_hat, axis=-1, keepdims=True)
+    for m in range(1, NB):
+        gain_copy(m).start()
+    gh_ref[...] = (dy_ref[...].astype(F32) + inv * (d_hat - x_hat * row_mean)).astype(BF16)
+    for m in range(1, NB):
+        ref = gains.at[tok_slot((hp + 4 - m // 2) % 4, (cp + m % 2) % 2)]
+        pltpu.make_async_remote_copy(
+            src_ref=ref, dst_ref=ref, send_sem=gain_send.at[m - 1], recv_sem=gain_recv.at[m - 1],
+            device_id=(hp, 1 - cp), device_id_type=MESH).wait_recv()
+    total = gains[0]
+    for d in range(1, NB):
+        total = total + gains[d]
+    gg_ref[...] = total
+    for m in range(1, NB):
+        gain_copy(m).wait_send()
+    for n in (NB - 2, NB - 1):
+        stage_out(n, n % 2).wait()
+    gkv.finish_sends()
+    ggq.finish_sends()
+
+
+def wq_kernel(ht_ref, gq_ref, gwo_in, gwq_ref, gwo_ref):
+    gwo_ref[...] = gwo_in[...]
+    b = gq_ref[0]
+
+    def rows(i, _):
+        r = pl.ds(pl.multiple_of(i * 2 * BLK, 2 * BLK), 2 * BLK)
+        gwq_ref[r, :] = dot(ht_ref[r, :], b)
+        return 0
+
+    lax.fori_loop(0, NB // 2, rows, 0)
 
 
 VMEM_SPEC = pl.BlockSpec(memory_space=pltpu.VMEM)
@@ -460,11 +634,12 @@
     return pl.pallas_call(
         backward_kernel,
         out_shape=(
-            jax.ShapeDtypeStruct((toks + 2 * BLK, hw), BF16),
+            jax.ShapeDtypeStruct((toks, hw), BF16),
+            jax.ShapeDtypeStruct((2 * BLK, hw), BF16),
             jax.ShapeDtypeStruct((NB, hw, toks), BF16),
         ),
         in_specs=[ANY_SPEC, ANY_SPEC] + [VMEM_SPEC] * 6,
-        out_specs=(VMEM_SPEC, ANY_SPEC),
+        out_specs=(VMEM_SPEC, VMEM_SPEC, ANY_SPEC),
         scratch_shapes=[
             pltpu.VMEM((NB, rows, width), BF16), pltpu.VMEM((hw, width), BF16),
             pltpu.VMEM((HEADS, toks, DH), BF16), pltpu.VMEM((DH, toks), BF16),
@@ -478,43 +653,64 @@
     )(dy_all, w_o, q, k, v, o_t, lse, tabs)
 
 
+def run_grads(gq, gkv, ot_all, dy_all, h_t, w_o, w_q, w_k, w_v, x_own, dy_own, gain):
+    rows, width = x_own.shape
+    toks = rows * NB
+    hw = HEADS * DH
+    kv = w_k.shape[1]
+    dma = pltpu.SemaphoreType.DMA
+    return pl.pallas_call(
+        grads_kernel,
+        out_shape=(
+            jax.ShapeDtypeStruct((rows, width), BF16), jax.ShapeDtypeStruct((rows, width), BF16),
+            jax.ShapeDtypeStruct((NB, toks, hw), BF16), jax.ShapeDtypeStruct((NB * hw, width), F32),
+            jax.ShapeDtypeStruct((width, kv), F32), jax.ShapeDtypeStruct((width, kv), F32),
+            jax.ShapeDtypeStruct((1, width), F32),
+        ),
+        in_specs=[ANY_SPEC] * 9 + [VMEM_SPEC] * 3,
+        out_specs=(VMEM_SPEC, VMEM_SPEC, ANY_SPEC, ANY_SPEC, VMEM_SPEC, VMEM_SPEC, VMEM_SPEC),
+        scratch_shapes=[
+            pltpu.VMEM((NB, 2 * BLK, hw), BF16), pltpu.VMEM((NB, hw, toks), BF16), pltpu.VMEM((NB, rows, width), BF16),
+            pltpu.VMEM((NB * hw, width), BF16), pltpu.VMEM((width, kv), BF16), pltpu.VMEM((width, kv), BF16),
+            pltpu.VMEM((2, NB * hw, BLK), F32), pltpu.VMEM((rows, width), F32), pltpu.VMEM((rows, NB * hw), BF16),
+            pltpu.VMEM((NB, rows, hw), BF16), pltpu.VMEM((toks, kv), BF16), pltpu.VMEM((toks, kv), BF16),
+            pltpu.VMEM((toks, hw), BF16), pltpu.VMEM((NB, 1, width), F32),
+            dma((10,)), dma((2,)), dma((NB,)),
+        ] + gather_sems() + gather_sems() + [dma((7,)), dma((7,))],
+        compiler_params=pltpu.CompilerParams(vmem_limit_bytes=60 * 1024 * 1024, collective_id=2, has_side_effects=True),
+        cost_estimate=pl.CostEstimate(flops=40_000_000_000, bytes_accessed=60_000_000, transcendentals=0),
+        name="grads",
+    )(gq, gkv, ot_all, dy_all, h_t.reshape(NB, BLK, toks), w_o, w_q, w_k, w_v, x_own, dy_own, gain)
+
+
+def run_wq(h_t, gq_all, gwo):
+    width, toks = h_t.shape
+    hw = HEADS * DH
+    cols = pl.BlockSpec((width, hw), lambda n: (0, n))
+    return pl.pallas_call(
+        wq_kernel,
+        grid=(NB,),
+        out_shape=(jax.ShapeDtypeStruct((width, NB * hw), F32), jax.ShapeDtypeStruct(gwo.shape, F32)),
+        in_specs=[VMEM_SPEC, pl.BlockSpec((1, toks, hw), lambda n: (n, 0, 0)), cols],
+        out_specs=(cols, cols),
+        compiler_params=pltpu.CompilerParams(vmem_limit_bytes=60 * 1024 * 1024),
+        cost_estimate=pl.CostEstimate(flops=17_000_000_000, bytes_accessed=67_000_000, transcendentals=0),
+        name="wq_grad",
+    )(h_t, gq_all, gwo)
+
+
 def solution(mesh):
     def device_step(hidden, grad_out, positions, norm_gain, w_q, w_k, w_v, w_o, inv_freq):
-        rows = hidden.shape[0]
-        toks = rows * NB
-        hw = HEADS * DH
-        hp, cp = lax.axis_index('hp'), lax.axis_index('cp')
-        me_tok = tok_slot(hp, cp)
         angles = positions.astype(F32)[:, None] * inv_freq[None, :]
         cos_h, sin_h = jnp.cos(angles), jnp.sin(angles)
         tab = jnp.concatenate([cos_h[:128], sin_h[:128], cos_h[128:], sin_h[128:]], axis=1)
         gain = norm_gain.astype(F32)[None, :]
         dy_all, h_t, q, k, v, o_t, lse, tabs = run_forward(hidden, grad_out, gain, w_q, w_k, w_v, tab)
-        gq_ext, ot_all = run_backward(dy_all, w_o, q, k, v, o_t, lse, tabs)
-        ot_all = ot_all.reshape(NB * hw, toks)
-        ext = lax.all_gather(gq_ext, ('hp', 'cp'), axis=0)
-        gq_cols = ext[:, :toks].transpose(1, 0, 2).reshape(toks, NB * hw)
-        gkv = ext[:, toks:].reshape(4, 2, 2 * BLK, 2, 2 * DH).transpose(0, 1, 3, 2, 4).reshape(4, toks, 2 * DH)
-        gk_cols = gkv[:, :, :DH].transpose(1, 0, 2).reshape(toks, 4 * DH)
-        gv_cols = gkv[:, :, DH:].transpose(1, 0, 2).reshape(toks, 4 * DH)
-        x_f32 = hidden.astype(F32)
-        inv_rms = lax.rsqrt(jnp.mean(x_f32 * x_f32, axis=-1, keepdims=True) + NORM_EPS)
-        x_hat = x_f32 * inv_rms
-        o_mine = lax.dynamic_slice_in_dim(ot_all, me_tok * rows, rows, 1)
-        output = (x_f32 + jnp.einsum('at,ab->tb', o_mine, w_o, preferred_element_type=F32)).astype(BF16)
-        grad_wo = jnp.dot(ot_all, dy_all.reshape(toks, -1), preferred_element_type=F32)
-        grad_wq = jnp.dot(h_t, gq_cols, preferred_element_type=F32)
-        grad_wk = jnp.dot(h_t, gk_cols, preferred_element_type=F32)
-        grad_wv = jnp.dot(h_t, gv_cols, preferred_element_type=F32)
-        mine = lambda a: lax.dynamic_slice_in_dim(a, me_tok * rows, rows, 0)
-        d_norm = (jnp.einsum('tb,ab->ta', mine(gq_cols), w_q, preferred_element_type=F32)
-                  + jnp.einsum('tb,ab->ta', mine(gk_cols), w_k, preferred_element_type=F32)
-                  + jnp.einsum('tb,ab->ta', mine(gv_cols), w_v, preferred_element_type=F32))
-        gain_part = jnp.sum(d_norm * x_hat, axis=0, keepdims=True)
-        grad_gain = jnp.sum(lax.all_gather(gain_part, ('cp', 'hp'), axis=0, tiled=True), axis=0)
-        d_hat = d_norm * gain
-        grad_hidden = (grad_out.astype(F32) + inv_rms * (d_hat - x_hat * jnp.mean(d_hat * x_hat, axis=-1, keepdims=True))).astype(BF16)
-        return output, grad_hidden, grad_wq, grad_wk, grad_wv, grad_wo, grad_gain
+        g_q, g_kv, ot_all = run_backward(dy_all, w_o, q, k, v, o_t, lse, tabs)
+        output, grad_hidden, gq_all, gwo, grad_wk, grad_wv, grad_gain = run_grads(
+            g_q, g_kv, ot_all, dy_all, h_t, w_o, w_q, w_k, w_v, hidden, grad_out, gain)
+        grad_wq, grad_wo = run_wq(h_t, gq_all, gwo)
+        return output, grad_hidden, grad_wq, grad_wk, grad_wv, grad_wo, grad_gain[0]
 
     seq_spec = P(('cp', 'hp'), None)
     whole = P()

time: 305 us -> 260 us (0.85)
  Pallas kernels: 133 us -> 248 us
  matrix products: 75.7 us -> 0 us
  local copies, waits for them, and re-layouts: 35.4 us -> 6.7 us
  waiting for transfers between devices: 27.3 us -> 0 us
  between operations: 14.2 us -> 0.7 us
  blocking collectives: 11 us -> 0 us
  other arithmetic: 7.7 us -> 3.9 us
    pallas_call x1 -> x3, Pallas kernels: 47.2 us -> 162 us  [the longest x1 82.5 us: run_grads(): pl.pallas_call(grads_kernel, out_shape=(jax.ShapeDtypeStruct((rows, width...]
    dot_general x8 -> x0, matrix products: 75.7 us -> none  [the longest x1 24.4 us: device_step(): grad_wq = jnp.dot(h_t, gq_cols, preferred_element_type=F32)]
    all_gather x1 -> x0, waiting for transfers between devices: 27.3 us -> none  [device_step(): ext = lax.all_gather(gq_ext, ('hp', 'cp'), axis=0)]
    all_gather x1 -> x0, blocking collectives: 11 us -> none  [device_step(): lax.all_gather(gain_part, ('cp', 'hp'), axis=0, tiled=True)]
    transpose x4 -> x0, local copies, waits for them, and re-layouts: 10.2 us -> none  [the longest x2 5.63 us: device_step(): gv_cols = gkv[:, :, DH:].transpose(1, 0, 2).reshape(toks, 4 * DH)]
    unnamed x24 -> x13, local copies, waits for them, and re-layouts: 16.1 us -> 6.68 us
    slice x2 -> x0, local copies, waits for them, and re-layouts: 9.05 us -> none  [the longest x1 7.32 us: device_step(): gq_cols = ext[:, :toks].transpose(1, 0, 2).reshape(toks, NB * hw)]
    convert_element_type x2 -> x0, other arithmetic: 4.17 us -> none  [the longest x1 2.88 us: device_step(): (grad_out.astype(F32) + inv_rms * (d_hat - x_hat * jnp.mean(d_hat * x_hat...]
  transfers between devices with their start and end apart: 1 -> 0, of which waited for: 1 -> 0; matrix products, arithmetic and copies ran while one was open for 9% -> 0% of each run, Pallas kernels for 0% -> 0%
where the time goes in v3:
time: 260 us; the launch traced here: 259 us
  Pallas kernels  248 us (95%)
  local copies, waits for them, and re-layouts  6.7 us (3%)
  other arithmetic  3.9 us (2%)
    pallas_call x1, Pallas kernels, run_forward(): pl.pallas_call(forward_kernel, out_shape=(jax.ShapeDtypeStruct((NB, rows,...  85.7 us
    pallas_call x1, Pallas kernels, run_grads(): pl.pallas_call(grads_kernel, out_shape=(jax.ShapeDtypeStruct((rows, width...  82.5 us
    pallas_call x1, Pallas kernels, run_backward(): pl.pallas_call(backward_kernel, out_shape=(jax.ShapeDtypeStruct((toks, hw...  47.2 us
    pallas_call x1, Pallas kernels, run_wq(): pl.pallas_call(wq_kernel, grid=(NB,), out_shape=(jax.ShapeDtypeStruct((wi...  32.7 us
    unnamed x13, local copies, waits for them, and re-layouts  6.68 us

profile of v3, /device:TPU:0, one launch (start us, length us, event | category | flops | bytes accessed | tf_op | source)
XLA Modules:
  0.0 259.4 jit_solution(7324347709025298082)
XLA Ops:
  0.6 0.7 convert_element_type.4
  1.3 1.3 broadcast_in_dim.9
  2.6 1.2 multiply_cosine_fusion
  3.8 0.8 pad_maximum_fusion.tab_own
  4.6 85.7 %attn_forward.1 = (bf16[8,256,2048]{2,1,0:T(8,128)(2,1)}, bf16[2048,2048]{1,0:T(8,128)(2,1)}, bf16[4,2048,64]{2,1,0:T(8,128)(2,1)}, bf16[2048,64]{1,0:T(8,128)(2...) custom-call(bf16[256,2048]{1,0:T(8,128)(2,1)} %x_ref.1, ...), custom_call_target="tpu_custom_call" | custom-call | flops 30000001024 | bytes 20000000 | tf_op jit(solution)/shard_map/attn_forward/pallas_call | solution.py:603
  90.3 47.2 %attn_backward.1 = (bf16[2048,256]{1,0:T(8,128)(2,1)}, bf16[512,256]{1,0:T(8,128)(2,1)}, bf16[8,256,2048]{2,1,0:T(8,128)(2,1)}) custom-call(bf16[8,256,2048]{2,1,0:T(8,128)(2,1)} %get-tuple-element.27.dy_all.dy_hbm, bf16[2048,2048]{1,0:T(8,128)(2,1)} %wo_hbm.3, bf16[4,2048,64]{2,1,0:T(8,128)(2,1)} %get-tuple-element.28.q_ref, ...), custom_call_target="tpu_custom_call" | custom-call | flops 40000000000 | bytes 20000000 | tf_op jit(solution)/shard_map/attn_backward/pallas_call | solution.py:634
  137.5 82.5 %grads.1 = (bf16[256,2048]{1,0:T(8,128)(2,1)}, bf16[256,2048]{1,0:T(8,128)(2,1)}, bf16[8,2048,256]{2,1,0:T(8,128)(2,1)}, f32[2048,2048]{1,0:T(8,128)}, f32[2048,...) custom-call(bf16[2048,256]{1,0:T(8,128)(2,1)} %get-tuple-element.34.gq_own, ...), custom_call_target="tpu_custom_call" | custom-call | flops 40000000000 | bytes 60000000 | tf_op jit(solution)/shard_map/grads/pallas_call | solution.py:662
  220.0 0.0 copy-start.2
  220.0 0.0 copy-start.1
  220.0 32.7 %wq_grad.1 = (f32[2048,2048]{1,0:T(8,128)}, f32[2048,2048]{1,0:T(8,128)}) custom-call(bf16[2048,2048]{1,0:T(8,128)(2,1)} %get-tuple-element.37.ht_ref, bf16[8,2048,256]{2,1,0:T(8,128)(2,1)} %get-tuple-element.40.gq_ref, f32[2048,2048]{1,0:T(8,128)} %get-tuple-element.41.gwo_in), custom_call_target="tpu_custom_call" | custom-call | flops 16999999488 | bytes 67000000 | tf_op jit(solution)/shard_map/wq_grad/pallas_call | solution.py:690
  252.7 0.0 copy-start
  252.7 0.0 copy-start.3
  252.7 2.5 copy.21
  255.2 0.0 copy-done.2
  255.2 1.0 copy.22
  256.2 0.0 copy-done.1
  256.2 1.3 copy.23
  257.5 0.0 copy-done
  257.5 1.3 copy.24
  258.8 0.0 copy-done.3
  258.8 0.6 copy.25
  (1 shorter events, 0.0 us)
Async XLA Ops:
  220.0 35.2 %copy-start.2 = (bf16[256,2048]{1,0:T(8,128)(2,1)S(1)}, bf16[256,2048]{1,0:T(8,128)(2,1)}, u32[]{:S(2)}) copy-start(bf16[256,2048]{1,0:T(8,128)(2,1)} %get-tuple-element.63) | copy-start | bytes 3145732
  220.0 36.2 %copy-start.1 = (f32[2048,256]{1,0:T(8,128)S(1)}, f32[2048,256]{1,0:T(8,128)}, u32[]{:S(2)}) copy-start(f32[2048,256]{1,0:T(8,128)} %get-tuple-element.65) | copy-start | bytes 6291460
  252.7 4.8 %copy-start = (f32[2048,256]{1,0:T(8,128)S(1)}, f32[2048,256]{1,0:T(8,128)}, u32[]{:S(2)}) copy-start(f32[2048,256]{1,0:T(8,128)} %get-tuple-element.66) | copy-start | bytes 6291460
  252.7 6.1 %copy-start.3 = (f32[1,2048]{1,0:T(1,128)S(1)}, f32[1,2048]{1,0:T(1,128)}, u32[]{:S(2)}) copy-start(f32[1,2048]{1,0:T(1,128)} %get-tuple-element.46) | copy-start | bytes 24580

commit v4 on v3

--- a/solution.py
+++ b/solution.py
@@ -219,7 +219,7 @@
 def forward_kernel(x_own, dy_own, gain_ref, wq_hbm, wk_hbm, wv_hbm, tab_own,
                    dy_all, ht_out, q_ref, k_ref, v_ref, ot_ref, lse_ref, tabs,
                    xg, ht, e_ref, m_ref, vt_ref, wq, wk, wv, wkv, stage,
-                   local_sem, tab_send, tab_recv, x_send, x_recv, dy_send, dy_recv):
+                   local_sem, t_send, t_recv, x_send, x_recv, dy_send, dy_recv):
     hp, cp, xn, yn, dn = neighbours()
     mine = tok_slot(hp, cp)
     hw = HEADS * DH
@@ -237,14 +237,8 @@
     gx = Gather(x_own, xg, tok_slot, x_send, x_recv, BLK)
     gdy = Gather(dy_own, dy_all, tok_slot, dy_send, dy_recv, BLK)
 
-    def table_copy(m):
-        to = ((hp + m // 2) % 4, (cp + m % 2) % 2)
-        return pltpu.make_async_remote_copy(
-            src_ref=tab_own, dst_ref=tabs.at[mine], send_sem=tab_send.at[m - 1], recv_sem=tab_recv.at[m - 1],
-            device_id=to, device_id_type=MESH)
-
-    for m in range(1, NB):
-        table_copy(m).start()
+    gt = Gather(tab_own, tabs, tok_slot, t_send, t_recv, 128)
+    gt.start_own()
     gx.start_own()
     for load in loads[1:4]:
         load.wait()
@@ -258,37 +252,36 @@
         loads[i].wait()
     dy_mine = pltpu.make_async_copy(stage, dy_all.at[mine], local_sem.at[6])
     dy_mine.start()
-    for m in range(1, NB):
-        src_slot = tok_slot((hp + 4 - m // 2) % 4, (cp + m % 2) % 2)
-        ref = tabs.at[src_slot]
-        pltpu.make_async_remote_copy(
-            src_ref=ref, dst_ref=ref, send_sem=tab_send.at[m - 1], recv_sem=tab_recv.at[m - 1],
-            device_id=(hp, 1 - cp), device_id_type=MESH).wait_recv()
-
     def project(e, _):
         @pl.when(e == 1)
         def _():
+            gt.await_sibling(3)
             gx.await_sibling(3)
 
         @pl.when(e == 2)
         def _():
+            gt.relay_near()
             gx.relay_near()
             gdy.start_own()
 
         @pl.when(e == 3)
         def _():
+            gt.await_sibling(4)
             gx.await_sibling(4)
 
         @pl.when(e == 5)
         def _():
+            gt.await_sibling(5)
             gx.await_sibling(5)
 
         @pl.when(e == 6)
         def _():
+            gt.relay_diagonal()
             gx.relay_diagonal()
 
         @pl.when(e == 7)
         def _():
+            gt.await_sibling(6)
             gx.await_sibling(6)
 
         m, b = e // 2, e % 2
@@ -304,13 +297,10 @@
     vt_ref[...] = v_ref[...].T
 
     def attend(j, _):
-        @pl.when(j == 5)
-        def _():
-            gdy.relay_near(range(0, CHUNKS // 2))
-
-        @pl.when(j == 6)
-        def _():
-            gdy.relay_near(range(CHUNKS // 2, CHUNKS))
+        for c in range(CHUNKS):
+            @pl.when(j == (1, 3, 4, 5)[c])
+            def _():
+                gdy.relay_near((c,))
 
         attend_block(j, q_ref, k_ref, vt_ref, e_ref, m_ref, ot_ref, lse_ref)
         return 0
@@ -319,8 +309,7 @@
     gdy.relay_diagonal()
     for number in (3, 4, 5, 6):
         gdy.await_sibling(number)
-    for m in range(1, NB):
-        table_copy(m).wait_send()
+    gt.finish_sends()
     gx.finish_sends()
     gdy.finish_sends()
     dy_mine.wait()
@@ -427,12 +416,7 @@
 
 
 def weight_grad(a_ref, b, stage):
-    def rows(i, _):
-        a = a_ref[pl.ds(2 * i, 2)].reshape(2 * BLK, NB * BLK)
-        stage[pl.ds(pl.multiple_of(i * 2 * BLK, 2 * BLK), 2 * BLK), :] = dot(a, b)
-        return 0
-
-    lax.fori_loop(0, NB // 2, rows, 0)
+    stage[...] = dot(a_ref[...].reshape(NB * BLK, NB * BLK), b)
 
 
 def grads_kernel(gq_own, gkv_own, ot_hbm, dy_hbm, ht_hbm, wo_hbm, wq_hbm, wk_hbm, wv_hbm, x_ref, dy_ref, gain_ref,
@@ -580,16 +564,11 @@
     ggq.finish_sends()
 
 
-def wq_kernel(ht_ref, gq_ref, gwo_in, gwq_ref, gwo_ref):
-    gwo_ref[...] = gwo_in[...]
-    b = gq_ref[0]
-
-    def rows(i, _):
-        r = pl.ds(pl.multiple_of(i * 2 * BLK, 2 * BLK), 2 * BLK)
-        gwq_ref[r, :] = dot(ht_ref[r, :], b)
-        return 0
-
-    lax.fori_loop(0, NB // 2, rows, 0)
+def wq_kernel(ht_ref, gq_ref, *refs):
+    ins, outs = refs[:len(refs) // 2], refs[len(refs) // 2 + 1:]
+    for src, dst in zip(ins, outs):
+        dst[...] = src[...]
+    refs[len(refs) // 2][...] = dot(ht_ref[...], gq_ref[0])
 
 
 VMEM_SPEC = pl.BlockSpec(memory_space=pltpu.VMEM)
@@ -619,8 +598,8 @@
             pltpu.VMEM((toks, CW), F32), pltpu.VMEM((NB, CW), F32), pltpu.VMEM((DH, toks), BF16),
             pltpu.VMEM((width, hw), BF16), pltpu.VMEM((width, 128), BF16), pltpu.VMEM((width, 128), BF16),
             pltpu.VMEM((width, 128), BF16), pltpu.VMEM((rows, width), BF16),
-            pltpu.SemaphoreType.DMA((8,)), pltpu.SemaphoreType.DMA((7,)), pltpu.SemaphoreType.DMA((7,)),
-        ] + gather_sems() + gather_sems(),
+            pltpu.SemaphoreType.DMA((8,)),
+        ] + gather_sems() + gather_sems() + gather_sems(),
         compiler_params=pltpu.CompilerParams(vmem_limit_bytes=60 * 1024 * 1024, collective_id=0, has_side_effects=True),
         cost_estimate=pl.CostEstimate(flops=30_000_000_000, bytes_accessed=20_000_000, transcendentals=0),
         name="attn_forward",
@@ -683,20 +662,21 @@
     )(gq, gkv, ot_all, dy_all, h_t.reshape(NB, BLK, toks), w_o, w_q, w_k, w_v, x_own, dy_own, gain)
 
 
-def run_wq(h_t, gq_all, gwo):
+def run_wq(h_t, gq_all, passed):
     width, toks = h_t.shape
     hw = HEADS * DH
     cols = pl.BlockSpec((width, hw), lambda n: (0, n))
+    specs = [cols] + [pl.BlockSpec((a.shape[0] // NB,) + a.shape[1:], lambda n: (n, 0)) for a in passed[1:]]
     return pl.pallas_call(
         wq_kernel,
         grid=(NB,),
-        out_shape=(jax.ShapeDtypeStruct((width, NB * hw), F32), jax.ShapeDtypeStruct(gwo.shape, F32)),
-        in_specs=[VMEM_SPEC, pl.BlockSpec((1, toks, hw), lambda n: (n, 0, 0)), cols],
-        out_specs=(cols, cols),
+        out_shape=(jax.ShapeDtypeStruct((width, NB * hw), F32),) + tuple(jax.ShapeDtypeStruct(a.shape, a.dtype) for a in passed),
+        in_specs=[VMEM_SPEC, pl.BlockSpec((1, toks, hw), lambda n: (n, 0, 0))] + specs,
+        out_specs=(cols,) + tuple(specs),
         compiler_params=pltpu.CompilerParams(vmem_limit_bytes=60 * 1024 * 1024),
         cost_estimate=pl.CostEstimate(flops=17_000_000_000, bytes_accessed=67_000_000, transcendentals=0),
         name="wq_grad",
-    )(h_t, gq_all, gwo)
+    )(h_t, gq_all, *passed)
 
 
 def solution(mesh):
@@ -709,7 +689,8 @@
         g_q, g_kv, ot_all = run_backward(dy_all, w_o, q, k, v, o_t, lse, tabs)
         output, grad_hidden, gq_all, gwo, grad_wk, grad_wv, grad_gain = run_grads(
             g_q, g_kv, ot_all, dy_all, h_t, w_o, w_q, w_k, w_v, hidden, grad_out, gain)
-        grad_wq, grad_wo = run_wq(h_t, gq_all, gwo)
+        grad_wq, grad_wo, output, grad_hidden, grad_wk, grad_wv = run_wq(
+            h_t, gq_all, (gwo, output, grad_hidden, grad_wk, grad_wv))
         return output, grad_hidden, grad_wq, grad_wk, grad_wv, grad_wo, grad_gain[0]
 
     seq_spec = P(('cp', 'hp'), None)

time: 260 us -> 251 us (0.965)
  local copies, waits for them, and re-layouts: 6.7 us -> 0.63 us
    unnamed x13 -> x3, local copies, waits for them, and re-layouts: 6.68 us -> 0.61 us
    pallas_call x1, Pallas kernels: 82.5 us -> 76.6 us  [run_grads(): pl.pallas_call(grads_kernel, out_shape=(jax.ShapeDtypeStruct((rows, width...]
where the time goes in v4:
time: 251 us
  Pallas kernels  246 us (98%)
  other arithmetic  3.9 us (2%)
    pallas_call x1, Pallas kernels, run_forward(): pl.pallas_call(forward_kernel, out_shape=(jax.ShapeDtypeStruct((NB, rows,...  87.1 us
    pallas_call x1, Pallas kernels, run_grads(): pl.pallas_call(grads_kernel, out_shape=(jax.ShapeDtypeStruct((rows, width...  76.6 us
    pallas_call x1, Pallas kernels, run_backward(): pl.pallas_call(backward_kernel, out_shape=(jax.ShapeDtypeStruct((toks, hw...  47.2 us
    pallas_call x1, Pallas kernels, run_wq(): pl.pallas_call(wq_kernel, grid=(NB,), out_shape=(jax.ShapeDtypeStruct((wi...  34.9 us

profile of v4, /device:TPU:0, one launch (start us, length us, event | category | flops | bytes accessed | tf_op | source)
XLA Modules:
  0.0 251.0 jit_solution(17692403656145840717)
XLA Ops:
  0.6 0.7 convert_element_type.4
  1.3 1.3 broadcast_in_dim.9
  2.6 1.2 multiply_cosine_fusion
  3.8 0.8 pad_maximum_fusion.tab_own
  4.6 87.1 %attn_forward.1 = (bf16[8,256,2048]{2,1,0:T(8,128)(2,1)}, bf16[2048,2048]{1,0:T(8,128)(2,1)}, bf16[4,2048,64]{2,1,0:T(8,128)(2,1)}, bf16[2048,64]{1,0:T(8,128)(2...) custom-call(bf16[256,2048]{1,0:T(8,128)(2,1)} %x_ref.1, ...), custom_call_target="tpu_custom_call" | custom-call | flops 30000001024 | bytes 20000000 | tf_op jit(solution)/shard_map/attn_forward/pallas_call | solution.py:582
  91.7 47.2 %attn_backward.1 = (bf16[2048,256]{1,0:T(8,128)(2,1)}, bf16[512,256]{1,0:T(8,128)(2,1)}, bf16[8,256,2048]{2,1,0:T(8,128)(2,1)}) custom-call(bf16[8,256,2048]{2,1,0:T(8,128)(2,1)} %get-tuple-element.32.dy_all.dy_hbm, bf16[2048,2048]{1,0:T(8,128)(2,1)} %wo_hbm.3, bf16[4,2048,64]{2,1,0:T(8,128)(2,1)} %get-tuple-element.33.q_ref, ...), custom_call_target="tpu_custom_call" | custom-call | flops 40000000000 | bytes 20000000 | tf_op jit(solution)/shard_map/attn_backward/pallas_call | solution.py:613
  138.9 76.6 %grads.1 = (bf16[256,2048]{1,0:T(8,128)(2,1)}, bf16[256,2048]{1,0:T(8,128)(2,1)}, bf16[8,2048,256]{2,1,0:T(8,128)(2,1)}, f32[2048,2048]{1,0:T(8,128)}, f32[2048,...) custom-call(bf16[2048,256]{1,0:T(8,128)(2,1)} %get-tuple-element.39.gq_own, ...), custom_call_target="tpu_custom_call" | custom-call | flops 40000000000 | bytes 60000000 | tf_op jit(solution)/shard_map/grads/pallas_call | solution.py:641
  215.5 0.0 copy-start
  215.5 34.9 %wq_grad.1 = (f32[2048,2048]{1,0:T(8,128)}, f32[2048,2048]{1,0:T(8,128)}, bf16[256,2048]{1,0:T(8,128)(2,1)}, bf16[256,2048]{1,0:T(8,128)(2,1)}, f32[2048,256]{1,0:T(8,128)}, /*index=5*/f32[2048,256]{1,0:T(8,128)}) custom-call(bf16[2048,2048]{1,0:T(8,128)(2,1)} %get-tuple-element.31.ht_ref, bf16[8,2048,256]{2,1,0:T(8,128)(2,1)} %get-tuple-element.42.gq_ref, ...), custom_call_target="tpu_custom_call" | custom-call | flops 16999999488 | bytes 67000000 | tf_op jit(solution)/shard_map/wq_grad/pallas_call | solution.py:670
  250.4 0.0 copy-done
  250.4 0.6 copy.17
  (1 shorter events, 0.0 us)
Async XLA Ops:
  215.5 35.0 %copy-start = (f32[1,2048]{1,0:T(1,128)S(1)}, f32[1,2048]{1,0:T(1,128)}, u32[]{:S(2)}) copy-start(f32[1,2048]{1,0:T(1,128)} %get-tuple-element.54) | copy-start | bytes 24580
